TPU v7x, 32 devices: a whole 2x2x4 slice. The times are simulated.
32 devices in a mesh: rep: 2 (over x), shard: 16 (over z, y, core).
Axes of the slice: x: 2, y: 2, z: 4, core: 2. Of those that a mesh axis runs over, the one named last changes fastest.
Arguments:
- dense: bfloat16 [8192, 128], P(('rep', 'shard')), may hold values from -6 to 6
- small_ids: int32 [8192, 32], P(('rep', 'shard')), may hold values from 0 to 511
- labels: int32 [8192], P(('rep', 'shard')), may hold values 0 or 1
- small_tables: bfloat16 [32, 512, 128], replicated, may hold values from -6 to 6
- large_tables: bfloat16 [16, 8192, 128], P('shard'), may hold values from -6 to 6
- batch_sizes: int32 [16, 32], replicated, may hold values from 1 to 128, as said below
- bag_ends: int32 [16, 32, 128], P('shard'), may hold values from 0 to 256, as said below
- owner_row_index: int32 [16, 32, 256], P('shard'), may hold values from 0 to 8191
- w_first: bfloat16 [1304, 1024], replicated, may hold values from -0.15625 to 0.15625
- b_first: float32 [1024], replicated, may hold values from -3 to 3
- w_out: float32 [1024], replicated, may hold values from -0.1875 to 0.1875
Outputs:
- small_new: bfloat16 [32, 512, 128], replicated
- large_new: bfloat16 [16, 8192, 128], P('shard')
Inputs may be any that keep to these rules, and one draw needn't show every extreme that they name: `batch_sizes`: every feature has some owner, and every owner some feature, with exactly 128. `bag_ends`: nondecreasing along the last dimension; bags j >= batch_sizes[f, d] are empty; some bag list reaches 256.
All inputs are finite; a program needn't handle non-finite values. No bound on the sum of `labels` on one device may be relied on, other than what follows from the above.
Results may differ from a plain program's by a relative error of at most 0.0095.
Values may be sent and summed in bfloat16 or wider, within the bound.
A program may use at most 192 MiB of HBM per device.

v0:
```python
import functools

import jax
import jax.numpy as jnp
from jax import lax
from jax.experimental import pallas as pl
from jax.experimental.pallas import tpu as pltpu
from jax.sharding import PartitionSpec as P

step_size = 32.0
LANES = 128
VMEM_LIMIT = 60 * 1024 * 1024
f32 = jnp.float32
bf16 = jnp.bfloat16


def whole(space):
    return pl.BlockSpec(memory_space=space)


def iota(shape, axis):
    return lax.broadcasted_iota(jnp.int32, shape, axis)


def members_of(ends, slots):
    span = ends.shape[-1]
    starts = jnp.where(iota((1, span), 1) == 0, 0, pltpu.roll(ends, 1, 1))
    places = iota((slots, span), 0)
    return ((places >= starts) & (places < ends)).astype(f32).astype(bf16)


def pool_kernel(
    first_ref, rows_ref, count_ref, ends_ref, table_ref, ids_ref, out_ref, by_table, by_sample,
    wide, picked,
):
    by_sample[...] = jnp.transpose(ids_ref[...])
    per_table = by_table.shape[0] // ids_ref.shape[0]
    for n in range(by_table.shape[0]):
        t = n // per_table
        by_table[n] = ids_ref[t : t + 1, :]
    slots = rows_ref.shape[1]
    owners = out_ref.shape[0]
    last = count_ref.shape[1] - 1
    first = first_ref[0]
    wide[...] = table_ref[...].astype(f32)
    picked[...] = jnp.zeros_like(picked)

    def owner(o, carry):
        d = o + first

        def group(g, c):
            base = pl.multiple_of(g * 8, 8)
            parts = [wide[pl.ds(rows_ref[d, base + u], 1), :] for u in range(8)]
            picked[pl.ds(pl.multiple_of(o * slots + base, 8), 8), :] = jnp.concatenate(parts, axis=0)
            return c

        return lax.fori_loop(0, (count_ref[d, last] + 7) // 8, group, carry)

    lax.fori_loop(0, owners, owner, 0)

    def sums(o, carry):
        members = members_of(ends_ref[pl.ds(o + first, 1), :], slots)
        block = picked[pl.ds(pl.multiple_of(o * slots, 8), slots), :].astype(bf16)
        pooled = lax.dot_general(
            members, block, (((0,), (0,)), ((), ())), preferred_element_type=f32
        )
        out_ref[o] = pooled.astype(bf16)
        return carry

    lax.fori_loop(0, owners, sums, 0, unroll=4)


def pool(first, owners, rows, ends, table, ids, devices):
    slots = rows.shape[1]
    width = table.shape[1]
    return pl.pallas_call(
        pool_kernel,
        out_shape=(
            jax.ShapeDtypeStruct((owners, ends.shape[1], width), bf16),
            jax.ShapeDtypeStruct((devices, 1, ids.shape[1]), ids.dtype),
            jax.ShapeDtypeStruct((ids.shape[1], ids.shape[0]), ids.dtype),
        ),
        in_specs=[whole(pltpu.SMEM)] * 3 + [whole(pltpu.VMEM)] * 3,
        out_specs=(whole(pltpu.VMEM),) * 3,
        scratch_shapes=[
            pltpu.VMEM(table.shape, f32),
            pltpu.VMEM((owners * slots, width), f32),
        ],
        compiler_params=pltpu.CompilerParams(vmem_limit_bytes=VMEM_LIMIT),
        name="pool",
    )(first, rows, ends, ends, table, ids)


def scatter_kernel(rows_ref, count_ref, ends_ref, fold_ref, table_ref, out_ref, spread, *sums):
    owners, slots = rows_ref.shape
    last = count_ref.shape[1] - 1
    lanes_of = len(sums)
    for total in sums:
        total[...] = jnp.zeros_like(total)

    def expand(d, carry):
        members = members_of(ends_ref[pl.ds(d, 1), :], slots)
        spread[pl.ds(pl.multiple_of(d * slots, 8), slots), :] = jnp.dot(
            members, fold_ref[d], preferred_element_type=f32
        )
        return carry

    lax.fori_loop(0, owners, expand, 0, unroll=4)

    def owner(d, carry):
        def group(g, c):
            base = pl.multiple_of(g * 8, 8)
            block = spread[pl.ds(pl.multiple_of(d * slots + base, 8), 8), :]
            for u in range(0, 8, lanes_of):
                spots = [rows_ref[d, base + u + v] for v in range(lanes_of)]
                news = [
                    sums[v][pl.ds(spots[v], 1), :] + block[u + v : u + v + 1]
                    for v in range(lanes_of)
                ]
                for v in range(lanes_of):
                    sums[v][pl.ds(spots[v], 1), :] = news[v]
            return c

        return lax.fori_loop(0, (count_ref[d, last] + 7) // 8, group, carry)

    lax.fori_loop(0, owners, owner, 0)
    step = 256

    def finish(g, c):
        at = pl.ds(pl.multiple_of(g * step, step), step)
        total = sums[0][at, :]
        for other in sums[1:]:
            total = total + other[at, :]
        out_ref[at, :] = (table_ref[at, :].astype(f32) - step_size * total).astype(bf16)
        return c

    lax.fori_loop(0, table_ref.shape[0] // step, finish, 0)


def scatter(rows, ends, fold, table):
    slots = rows.shape[1]
    return pl.pallas_call(
        scatter_kernel,
        out_shape=jax.ShapeDtypeStruct(table.shape, bf16),
        in_specs=[whole(pltpu.SMEM), whole(pltpu.SMEM)] + [whole(pltpu.VMEM)] * 3,
        out_specs=whole(pltpu.VMEM),
        scratch_shapes=[pltpu.VMEM((rows.size, table.shape[1]), f32)]
        + [pltpu.VMEM(table.shape, f32)] * 4,
        compiler_params=pltpu.CompilerParams(vmem_limit_bytes=VMEM_LIMIT),
        cost_estimate=pl.CostEstimate(
            flops=20 * table.size * LANES, bytes_accessed=4 * table.size, transcendentals=0
        ),
        name="scatter",
    )(rows, ends, ends, fold, table)


def small_kernel(part_rows, first_ref, ids_ref, grads_ref, table_ref, out_ref):
    senders, batch = ids_ref.shape
    rows = iota((part_rows, batch), 0) + first_ref[0]
    total = jnp.zeros(out_ref.shape, f32)

    def one(s, total):
        hot = (rows == ids_ref[pl.ds(s, 1), :]).astype(f32).astype(bf16)
        return total + jnp.dot(hot, grads_ref[s], preferred_element_type=f32)

    total = lax.fori_loop(0, senders, one, total, unroll=8)
    out_ref[...] = (table_ref[...].astype(f32) - step_size * total).astype(bf16)


def small_update(first, ids, grads, rows):
    return pl.pallas_call(
        functools.partial(small_kernel, rows.shape[0]),
        out_shape=jax.ShapeDtypeStruct(rows.shape, bf16),
        in_specs=[whole(pltpu.SMEM)] + [whole(pltpu.VMEM)] * 3,
        out_specs=whole(pltpu.VMEM),
        compiler_params=pltpu.CompilerParams(vmem_limit_bytes=VMEM_LIMIT),
        name="small_update",
    )(first, ids, grads, rows)


def spans_of(vec_count):
    return [(i, i * (i - 1) // 2) for i in range(1, vec_count)]


def top_kernel(
    vec_count, pad, index_ref, sizes_ref, dense_ref, labels_ref, small_ref, large_ref,
    w_ref, bias_ref, wout_ref, small_out, fold_out, vecs, gram, pairs, spread,
):
    batch, width = dense_ref.shape
    small_count = small_ref.shape[0]
    feats, bag_span = large_ref.shape[0], large_ref.shape[1]
    pair_pad = pairs.shape[1]
    pair_count = vec_count * (vec_count - 1) // 2
    scale = width ** (-0.5)
    spans = spans_of(vec_count)

    def rows_of(i):
        return pl.ds(i, batch, stride=pad)

    vecs[rows_of(0), :] = dense_ref[...].astype(f32)
    for t in range(small_count):
        vecs[rows_of(1 + t), :] = small_ref[t].astype(f32)
    sample = iota((batch, bag_span), 0)
    bag = iota((batch, bag_span), 1) * batch
    for f in range(feats):
        reach = sample * sizes_ref[f, index_ref[0]]
        hot = ((reach >= bag) & (reach < bag + batch)).astype(f32).astype(bf16)
        vecs[rows_of(1 + small_count + f), :] = jnp.dot(
            hot, large_ref[f], preferred_element_type=f32
        )
    for i in range(vec_count, pad):
        vecs[rows_of(i), :] = jnp.zeros((batch, width), f32)

    unroll = 8

    def gram_step(g, c):
        for u in range(unroll):
            at = pl.ds(pl.multiple_of((g * unroll + u) * pad, 8), pad)
            own = vecs[at, :].astype(bf16)
            gram[at, 0:pad] = lax.dot_general(
                own, own, (((1,), (1,)), ((), ())), preferred_element_type=f32
            )
        return c

    lax.fori_loop(0, batch // unroll, gram_step, 0)

    lane = iota((1, LANES), 1)
    chunk = 64
    for start in range(0, batch, chunk):
        tile = jnp.zeros((chunk, LANES), f32)
        at_tile = 0
        for i, off in spans:
            piece = gram[pl.ds(start * pad + i, chunk, stride=pad), :]
            turn = off % LANES
            if turn:
                piece = pltpu.roll(piece, turn, 1)
            low = off - at_tile * LANES
            tile = jnp.where((lane >= low) & (lane < low + i), piece, tile)
            if low + i >= LANES:
                pairs[start : start + chunk, at_tile * LANES : (at_tile + 1) * LANES] = (
                    tile * scale
                ).astype(bf16)
                at_tile += 1
                rest = low + i - LANES
                tile = jnp.where(lane < rest, piece, jnp.zeros_like(piece))
        if at_tile * LANES < pair_pad:
            pairs[start : start + chunk, at_tile * LANES : pair_pad] = (tile * scale).astype(bf16)

    block = 128
    labels_col = jnp.transpose(
        jnp.broadcast_to(labels_ref[...].astype(f32), (LANES, batch))
    )[:, 0:1]
    for start in range(0, batch, block):
        at = slice(start, start + block)
        preact = (
            jnp.dot(pairs[at, :], w_ref[0:pair_pad, :], preferred_element_type=f32)
            + jnp.dot(dense_ref[at, :], w_ref[pair_count : pair_count + width, :], preferred_element_type=f32)
            + bias_ref[...]
        )
        squash = jax.nn.sigmoid(preact)
        logits = jnp.sum(preact * squash * wout_ref[...], axis=1, keepdims=True)
        grad = jax.nn.sigmoid(logits) - labels_col[at, :]
        pre_grad = (
            grad * wout_ref[...] * (squash * (1.0 + preact * (1.0 - squash)))
        ).astype(bf16)
        for q in range(0, pair_pad, LANES):
            spread[at, q : q + LANES] = lax.dot_general(
                pre_grad, w_ref[q : q + LANES, :], (((1,), (1,)), ((), ())),
                preferred_element_type=f32,
            ) * scale

    gram[rows_of(0), :] = jnp.zeros((batch, LANES), f32)
    for i in range(vec_count, pad):
        gram[rows_of(i), :] = jnp.zeros((batch, LANES), f32)
    for start in range(0, batch, chunk):
        for i, off in spans:
            first = off // LANES
            low = off - first * LANES
            here = spread[start : start + chunk, first * LANES : (first + 1) * LANES]
            if low + i > LANES:
                after = spread[start : start + chunk, (first + 1) * LANES : (first + 2) * LANES]
                here = jnp.where(lane >= low, here, after)
            if low:
                here = pltpu.roll(here, LANES - low, 1)
            gram[pl.ds(start * pad + i, chunk, stride=pad), :] = jnp.where(lane < i, here, 0.0)

    def back_step(g, c):
        for u in range(unroll):
            at = pl.ds(pl.multiple_of((g * unroll + u) * pad, 8), pad)
            lower = gram[at, :]
            both = lower[:, 0:pad] + jnp.transpose(lower)[0:pad, :]
            vecs[at, :] = jnp.dot(
                both.astype(bf16), vecs[at, :].astype(bf16), preferred_element_type=f32
            )
        return c

    lax.fori_loop(0, batch // unroll, back_step, 0)

    for t in range(small_count):
        small_out[t] = vecs[rows_of(1 + t), :].astype(bf16)
    sample_lane = iota((bag_span, batch), 1)
    bag_row = iota((bag_span, batch), 0) * batch
    for f in range(feats):
        reach = sample_lane * sizes_ref[f, index_ref[0]]
        hot = ((reach >= bag_row) & (reach < bag_row + batch)).astype(f32).astype(bf16)
        fold_out[f] = jnp.dot(
            hot, vecs[rows_of(1 + small_count + f), :].astype(bf16), preferred_element_type=f32
        ).astype(bf16)


def top(index, sizes, dense, labels, small, large, w_first, bias, wout):
    batch, width = dense.shape
    small_count, feats, bag_span = small.shape[0], large.shape[0], large.shape[1]
    vec_count = 1 + small_count + feats
    pad = -(-vec_count // 8) * 8
    pair_count = vec_count * (vec_count - 1) // 2
    pair_pad = -(-pair_count // LANES) * LANES
    return pl.pallas_call(
        functools.partial(top_kernel, vec_count, pad),
        out_shape=(
            jax.ShapeDtypeStruct((small_count, batch, width), bf16),
            jax.ShapeDtypeStruct((feats, bag_span, width), bf16),
        ),
        in_specs=[whole(pltpu.SMEM)] * 2 + [whole(pltpu.VMEM)] * 7,
        out_specs=(whole(pltpu.VMEM), whole(pltpu.VMEM)),
        scratch_shapes=[
            pltpu.VMEM((batch * pad, width), f32),
            pltpu.VMEM((batch * pad, LANES), f32),
            pltpu.VMEM((batch, pair_pad), bf16),
            pltpu.VMEM((batch, pair_pad), f32),
        ],
        compiler_params=pltpu.CompilerParams(vmem_limit_bytes=VMEM_LIMIT),
        name="top",
    )(
        index, sizes, dense, labels[None, :], small, large, w_first,
        bias[None, :], wout[None, :],
    )


def greet_all():
    copies, groups = lax.axis_size("rep"), lax.axis_size("shard")
    devices = copies * groups
    index = lax.axis_index("rep") * groups + lax.axis_index("shard")
    barrier = pltpu.get_barrier_semaphore()

    def greet(k, c):
        other = lax.rem(index + k, devices)
        pl.semaphore_signal(
            barrier, inc=1, device_id={"rep": other // groups, "shard": lax.rem(other, groups)},
            device_id_type=pl.DeviceIdType.MESH,
        )
        return c

    lax.fori_loop(1, devices, greet, 0)
    pl.semaphore_wait(barrier, devices - 1)


def remote(src, dst, send, recv, rep, shard):
    return pltpu.make_async_remote_copy(
        src_ref=src, dst_ref=dst, send_sem=send, recv_sem=recv,
        device_id={"rep": rep, "shard": shard}, device_id_type=pl.DeviceIdType.MESH,
    )


def forward_kernel(
    pooled_ref, ids_ref, own_ids_ref, tables_ref, large_out, ids_out, small_out,
    send, recv, id_send, id_recv, own, tables,
):
    copies, groups = lax.axis_size("rep"), lax.axis_size("shard")
    devices = copies * groups
    rep, me = lax.axis_index("rep"), lax.axis_index("shard")
    index = rep * groups + me

    def block(k):
        to = lax.rem(me + k, groups)
        return remote(pooled_ref.at[to], large_out.at[me], send.at[k], recv.at[k], rep, to)

    def ids(k):
        to = lax.rem(index + k, devices)
        return remote(
            ids_ref.at[to], ids_out.at[index], id_send.at[k], id_recv.at[k],
            to // groups, lax.rem(to, groups),
        )

    def block_in(k):
        at = lax.rem(me + groups - k, groups)
        return remote(pooled_ref.at[at], large_out.at[at], send.at[k], recv.at[k], rep, at)

    def ids_in(k):
        at = lax.rem(index + devices - k, devices)
        return remote(
            ids_ref.at[at], ids_out.at[at], id_send.at[k], id_recv.at[k],
            at // groups, lax.rem(at, groups),
        )

    def run(low, high, act):
        def body(k, c):
            act(k)
            return c

        lax.fori_loop(low, high, body, 0)

    fetch = pltpu.make_async_copy(tables_ref, tables, own.at[2])
    fetch.start()
    greet_all()
    run(1, groups, lambda k: block(k).start())
    run(1, devices, lambda k: ids(k).start())
    mine = pltpu.make_async_copy(pooled_ref.at[me], large_out.at[me], own.at[0])
    mine_ids = pltpu.make_async_copy(ids_ref.at[index], ids_out.at[index], own.at[1])
    mine.start()
    mine_ids.start()
    batch, small_count = own_ids_ref.shape
    rows = iota((batch, tables_ref.shape[1]), 1)
    fetch.wait()
    for t in range(small_count):
        hot = (own_ids_ref[:, t : t + 1] == rows).astype(f32).astype(bf16)
        small_out[t] = jnp.dot(hot, tables[t], preferred_element_type=f32).astype(bf16)
    mine.wait()
    mine_ids.wait()
    run(1, groups, lambda k: block_in(k).wait_recv())
    run(1, devices, lambda k: ids_in(k).wait_recv())
    run(1, groups, lambda k: block(k).wait_send())
    run(1, devices, lambda k: ids(k).wait_send())


def forward(pooled, ids, own_ids, tables):
    groups, devices = pooled.shape[0], ids.shape[0]
    return pl.pallas_call(
        forward_kernel,
        out_shape=(
            jax.ShapeDtypeStruct(pooled.shape, pooled.dtype),
            jax.ShapeDtypeStruct(ids.shape, ids.dtype),
            jax.ShapeDtypeStruct(
                (tables.shape[0], own_ids.shape[0], tables.shape[2]), tables.dtype
            ),
        ),
        in_specs=[whole(pltpu.VMEM)] * 3 + [whole(pl.ANY)],
        out_specs=(whole(pltpu.VMEM),) * 3,
        scratch_shapes=[pltpu.SemaphoreType.DMA((groups,))] * 2
        + [pltpu.SemaphoreType.DMA((devices,))] * 2
        + [pltpu.SemaphoreType.DMA((3,)), pltpu.VMEM(tables.shape, tables.dtype)],
        compiler_params=pltpu.CompilerParams(
            collective_id=0, has_side_effects=True, vmem_limit_bytes=VMEM_LIMIT
        ),
        name="forward",
    )(pooled, ids, own_ids, tables)


def fold_kernel(fold_ref, out_ref, send, recv, far_send, far_recv, own):
    copies, groups = lax.axis_size("rep"), lax.axis_size("shard")
    rep, me = lax.axis_index("rep"), lax.axis_index("shard")
    other = 1 - rep

    def out_block(k):
        to = lax.rem(me + k, groups)
        return remote(
            fold_ref.at[to], out_ref.at[rep * groups + me], send.at[k], recv.at[k], rep, to
        )

    def in_block(k):
        at = lax.rem(me + groups - k, groups)
        return remote(
            fold_ref.at[at], out_ref.at[rep * groups + at], send.at[k], recv.at[k], rep, at
        )

    def far_out(k):
        slot = out_ref.at[rep * groups + lax.rem(me + groups - k, groups)]
        return remote(slot, slot, far_send.at[k], far_recv.at[k], other, me)

    def far_in(k):
        slot = out_ref.at[other * groups + lax.rem(me + groups - k, groups)]
        return remote(slot, slot, far_send.at[k], far_recv.at[k], other, me)

    own_far = remote(
        fold_ref.at[me], out_ref.at[rep * groups + me], far_send.at[0], far_recv.at[0], other, me
    )

    def run(act):
        def body(k, c):
            act(k)
            return c

        lax.fori_loop(1, groups, body, 0)

    greet_all()
    run(lambda k: out_block(k).start())
    own_far.start()
    mine = pltpu.make_async_copy(fold_ref.at[me], out_ref.at[rep * groups + me], own.at[0])
    mine.start()

    def pass_on(k):
        in_block(k).wait_recv()
        far_out(k).start()

    run(pass_on)
    mine.wait()
    far_in(0).wait_recv()
    run(lambda k: far_in(k).wait_recv())
    own_far.wait_send()
    run(lambda k: far_out(k).wait_send())
    run(lambda k: out_block(k).wait_send())


def fold_exchange(fold, copies):
    groups = fold.shape[0]
    return pl.pallas_call(
        fold_kernel,
        out_shape=jax.ShapeDtypeStruct((copies * groups,) + fold.shape[1:], fold.dtype),
        in_specs=[whole(pltpu.VMEM)],
        out_specs=whole(pltpu.VMEM),
        scratch_shapes=[pltpu.SemaphoreType.DMA((groups,))] * 4 + [pltpu.SemaphoreType.DMA((1,))],
        compiler_params=pltpu.CompilerParams(
            collective_id=1, has_side_effects=True, vmem_limit_bytes=VMEM_LIMIT
        ),
        cost_estimate=pl.CostEstimate(
            flops=400 * fold.size * LANES, bytes_accessed=4 * fold.size, transcendentals=0
        ),
        name="fold_exchange",
    )(fold)


def spread_kernel(own_ref, out_ref, send_z, send_1, send_2, send_core, recv, local):
    groups = lax.axis_size("shard")
    ring = groups // 4
    rep, member = lax.axis_index("rep"), lax.axis_index("shard")
    z, y, core = member // 4, lax.rem(member, 4) // 2, lax.rem(member, 2)

    def shard_of(z_at, y_at, core_at):
        return z_at * 4 + y_at * 2 + core_at

    def send(h, src, rep_at, z_at, y_at, sem, to_rep, to_z, to_y, to_core):
        slot = rep_at * groups + shard_of(z_at, y_at, core)
        source = out_ref.at[slot, h] if src is None else src
        return remote(
            source, out_ref.at[slot, h], sem, recv.at[h, slot],
            to_rep, shard_of(to_z, to_y, to_core),
        )

    def arrived(h, rep_at, z_at, y_at, core_at):
        slot = rep_at * groups + shard_of(z_at, y_at, core_at)
        place = out_ref.at[slot, h]
        remote(place, place, local.at[1], recv.at[h, slot], rep, member).wait_recv()

    greet_all()
    pending = []

    def go(copy):
        copy.start()
        pending.append(copy)

    def second(h, k, src, rep_at, z_at, y_at):
        hop = (rep, z, 1 - y, core) if h == 0 else (1 - rep, z, y, core)
        go(send(h, src, rep_at, z_at, y_at, send_1.at[h, k], *hop))

    def third(h, k, src, rep_at, z_at, y_at):
        hop = (1 - rep, z, y, core) if h == 0 else (rep, z, 1 - y, core)
        go(send(h, src, rep_at, z_at, y_at, send_2.at[h, k], *hop))

    def last(h, k, src, rep_at, z_at, y_at):
        go(send(h, src, rep_at, z_at, y_at, send_core.at[h, k], rep, z, y, 1 - core))

    for k in range(1, ring):
        for h in range(2):
            go(send(h, own_ref.at[h], rep, z, y, send_z.at[h, k], rep, lax.rem(z + k, ring), y, core))
    for h in range(2):
        src = own_ref.at[h]
        second(h, 0, src, rep, z, y)
        third(h, 0, src, rep, z, y)
        last(h, 0, src, rep, z, y)
    mine = pltpu.make_async_copy(
        own_ref, out_ref.at[rep * groups + member], local.at[0]
    )
    mine.start()
    for k in range(1, ring):
        z_at = lax.rem(z + ring - k, ring)
        for h in range(2):
            arrived(h, rep, z_at, y, core)
            second(h, k, None, rep, z_at, y)
            third(h, k, None, rep, z_at, y)
            last(h, k, None, rep, z_at, y)
    for k in range(ring):
        z_at = lax.rem(z + ring - k, ring)
        for h in range(2):
            where = (rep, z_at, 1 - y) if h == 0 else (1 - rep, z_at, y)
            arrived(h, *where, core)
            third(h, ring + k, None, *where)
            last(h, ring + k, None, *where)
    for k in range(2 * ring):
        z_at = lax.rem(z + ring - k % ring, ring)
        for h in range(2):
            if h == 0:
                where = (1 - rep, z_at, y if k < ring else 1 - y)
            else:
                where = (rep if k < ring else 1 - rep, z_at, 1 - y)
            arrived(h, *where, core)
            last(h, 2 * ring + k, None, *where)
    for r in range(2):
        for k in range(ring):
            for y_at in range(2):
                for h in range(2):
                    arrived(h, r, k, y_at, 1 - core)
    mine.wait()
    for copy in pending:
        copy.wait_send()


def spread_all(own, copies, groups):
    rows, width = own.shape
    ring = groups // 4
    devices = copies * groups
    out = pl.pallas_call(
        spread_kernel,
        out_shape=jax.ShapeDtypeStruct((devices, 2, rows // 2, width), own.dtype),
        in_specs=[whole(pltpu.VMEM)],
        out_specs=whole(pltpu.VMEM),
        scratch_shapes=[
            pltpu.SemaphoreType.DMA((2, ring)),
            pltpu.SemaphoreType.DMA((2, ring)),
            pltpu.SemaphoreType.DMA((2, 2 * ring)),
            pltpu.SemaphoreType.DMA((2, 4 * ring)),
            pltpu.SemaphoreType.DMA((2, devices)),
            pltpu.SemaphoreType.DMA((2,)),
        ],
        compiler_params=pltpu.CompilerParams(
            collective_id=2, has_side_effects=True, vmem_limit_bytes=VMEM_LIMIT
        ),
        name="spread_all",
    )(own.reshape(2, rows // 2, width))
    return out.reshape(devices * rows, width)


def shards(
    dense, small_ids, labels, small_tables, large_tables, batch_sizes, bag_ends,
    owner_row_index, w_first, b_first, w_out,
):
    groups = lax.axis_size("shard")
    copies = lax.axis_size("rep")
    devices = groups * copies
    first = lax.axis_index("rep") * groups
    index = first + lax.axis_index("shard")
    small_count, small_rows, width = small_tables.shape
    per_table = devices // small_count
    ends, rows, table = bag_ends[0], owner_row_index[0], large_tables[0]

    pooled, sent_ids, own_ids = pool(
        first[None], groups, rows, ends, table, jnp.transpose(small_ids), devices
    )
    large, all_ids, small = forward(pooled, sent_ids, own_ids, small_tables)
    small_grads, fold = top(
        index[None], batch_sizes, dense, labels, small, large, w_first, b_first, w_out
    )
    fold_all = fold_exchange(fold, copies)
    sent = jnp.repeat(small_grads, per_table, axis=0)
    sent, fold_all = lax.optimization_barrier((sent, fold_all))
    arrived = lax.all_to_all(sent, ("rep", "shard"), split_axis=0, concat_axis=0, tiled=True)
    large_new = scatter(rows, ends, fold_all, table)
    part_rows = small_count * small_rows // devices
    flat = small_tables.reshape(small_count * small_rows, width)
    own = lax.dynamic_slice_in_dim(flat, index * part_rows, part_rows, 0)
    first_row = (lax.rem(index, per_table) * part_rows)[None].astype(jnp.int32)
    updated = small_update(first_row, all_ids[:, 0], arrived, own)
    small_new = spread_all(updated, copies, groups).reshape(small_count, small_rows, width)
    return small_new, large_new[None]


def solution(mesh):
    both = ("rep", "shard")
    placed = (
        P(both, None), P(both, None), P(both), P(), P("shard", None, None), P(),
        P("shard", None, None), P("shard", None, None), P(), P(), P(),
    )
    return jax.shard_map(
        shards, mesh=mesh, in_specs=placed, out_specs=(P(), P("shard", None, None)), check_vma=False
    )
```

profile of v0, /device:TPU:1, one launch (start us, length us, event | category | flops | bytes accessed | tf_op | source)
XLA Modules:
  0.0 186.8 jit_solution(6390055693599351718)
XLA Ops:
  0.6 14.8 %pool.1 = (bf16[16,128,128]{2,1,0:T(8,128)(2,1)}, s32[32,1,256]{2,1,0:T(1,128)}, s32[256,32]{1,0:T(8,128)}) custom-call(s32[1]{0:T(128)} %bitcast.first_ref, s32[32,256]{1,0:T(8,128)} %bitcast.27, s32[32,128]{1,0:T(8,128)} %bitcast.22, s32[32,128]{1,0:T(8,128)} %bitcast.23, bf16[8192,128]{1,0:T(8,128)(2,1)} %bitcast.18, s32[32,256]{1,0:T(8,128)} %bitcast.26), custom_call_target="tpu_custom_call" | custom-call | tf_op jit(solution)/shard_map/pool/pallas_call | solution.py:76
  15.4 22.5 %forward.1 = (bf16[16,128,128]{2,1,0:T(8,128)(2,1)}, s32[32,1,256]{2,1,0:T(1,128)}, bf16[32,256,128]{2,1,0:T(8,128)(2,1)}) custom-call(bf16[16,128,128]{2,1,0:T(8,128)(2,1)} %get-tuple-element.12.pooled_ref, s32[32,1,256]{2,1,0:T(1,128)} %get-tuple-element.13.ids_ref, s32[256,32]{1,0:T(8,128)} %get-tuple-element.14.own_ids_ref, bf16[32,512,128]{2,1,0:T(8,128)(2,1)} %tables_ref.1), custom_call_target="tpu_custom_call" | custom-call | tf_op jit(solution)/shard_map/forward/pallas_call | solution.py:428
  37.9 26.9 %top.1 = (bf16[32,256,128]{2,1,0:T(8,128)(2,1)}, bf16[16,128,128]{2,1,0:T(8,128)(2,1)}) custom-call(s32[1]{0:T(128)} %bitcast.5.index_ref, s32[16,32]{1,0:T(8,128)} %sizes_ref.1, bf16[256,128]{1,0:T(8,128)(2,1)} %dense_ref.1, s32[1,256]{1,0:T(1,128)} %bitcast.31, bf16[32,256,128]{2,1,0:T(8,128)(2,1)} %get-tuple-element.16.small_ref, ...), custom_call_target="tpu_custom_call" | custom-call | tf_op jit(solution)/shard_map/top/pallas_call | solution.py:318
  64.8 23.9 %fold_exchange.1.fold_ref = bf16[32,128,128]{2,1,0:T(8,128)(2,1)} custom-call(bf16[16,128,128]{2,1,0:T(8,128)(2,1)} %get-tuple-element.19.fold_ref), custom_call_target="tpu_custom_call" | custom-call | flops 13421772800 | bytes 1048576 | tf_op jit(solution)/shard_map/fold_exchange/pallas_call | solution.py:506
  88.7 0.0 copy-start.1
  88.7 6.3 %all-to-all-start = ((bf16[32,256,128]{2,1,0:T(8,128)(2,1)}), bf16[32,256,128]{2,1,0:T(8,128)(2,1)S(1)}, u32[]{:S(2)}, u32[]{:S(2)}) async-start(bf16[32,256,128]{2,1,0:T(8,128)(2,1)} %get-tuple-element.20), calls=%async_computation | async-start | bytes 4194304 | tf_op jit(solution)/shard_map/all_to_all | solution.py:655
  95.0 0.0 copy-done.1
  95.0 0.6 copy.15
  95.6 1.6 constant_dynamic-slice_fusion.table_ref
  97.2 22.9 %scatter.1 = bf16[8192,128]{1,0:T(8,128)(2,1)} custom-call(s32[32,256]{1,0:T(8,128)} %bitcast.28, s32[32,128]{1,0:T(8,128)} %bitcast.24, s32[32,128]{1,0:T(8,128)} %bitcast.25, bf16[32,128,128]{2,1,0:T(8,128)(2,1)} %fold_exchange.1.fold_ref, bf16[8192,128]{1,0:T(8,128)(2,1)} %bitcast.19), custom_call_target="tpu_custom_call" | custom-call | flops 2684354560 | bytes 4194304 | tf_op jit(solution)/shard_map/scatter/pallas_call | solution.py:142
  120.1 24.3 %all-to-all-done.grads_ref = bf16[32,256,128]{2,1,0:T(8,128)(2,1)S(1)} async-done(((bf16[32,256,128]{2,1,0:T(8,128)(2,1)}), bf16[32,256,128]{2,1,0:T(8,128)(2,1)S(1)}, u32[]{:S(2)}, u32[]{:S(2)}) %all-to-all-start) | async-done | bytes 2097184 | tf_op jit(solution)/shard_map/all_to_all | solution.py:655
  144.3 0.0 copy-start
  144.3 1.3 copy-done
  145.7 5.2 %small_update.1 = bf16[512,128]{1,0:T(8,128)(2,1)} custom-call(s32[1]{0:T(128)} %constant.7.clone.1.first_ref, s32[32,256]{1,0:T(8,128)} %bitcast.21, bf16[32,256,128]{2,1,0:T(8,128)(2,1)} %copy-done, bf16[512,128]{1,0:T(8,128)(2,1)} %constant_dynamic-slice_fusion.table_ref), custom_call_target="tpu_custom_call" | custom-call | tf_op jit(solution)/shard_map/small_update/pallas_call | solution.py:171
  150.8 31.3 %spread_all.1 = bf16[32,2,256,128]{3,2,1,0:T(8,128)(2,1)} custom-call(bf16[2,256,128]{2,1,0:T(8,128)(2,1)} %bitcast.20), custom_call_target="tpu_custom_call" | custom-call | tf_op jit(solution)/shard_map/spread_all/pallas_call | solution.py:611
  182.1 4.7 %copy.17 = bf16[32,512,128]{2,1,0:T(8,128)(2,1)} copy(bf16[32,512,128]{2,1,0:T(8,128)(2,1)} %bitcast.16) | data formatting | bytes 8388608
Async XLA Ops:
  88.7 6.3 %copy-start.1 = (s32[32,1,256]{2,1,0:T(1,128)S(1)}, s32[32,1,256]{2,1,0:T(1,128)}, u32[]{:S(2)}) copy-start(s32[32,1,256]{2,1,0:T(1,128)} %get-tuple-element.15) | copy-start | bytes 98308
  88.7 55.7 %all-to-all-start = ((bf16[32,256,128]{2,1,0:T(8,128)(2,1)}), bf16[32,256,128]{2,1,0:T(8,128)(2,1)S(1)}, u32[]{:S(2)}, u32[]{:S(2)}) async-start(bf16[32,256,128]{2,1,0:T(8,128)(2,1)} %get-tuple-element.20), calls=%async_computation | async-start | bytes 4194304 | tf_op jit(solution)/shard_map/all_to_all | solution.py:655
  144.3 1.3 copy-start
where the time goes:
time: 188 us; the launch traced here: 187 us
  Pallas kernels  147 us (78%)
  waiting for transfers between devices  24.3 us (13%)
  local copies, waits for them, and re-layouts  8.14 us (4%)
  starting transfers between devices  6.32 us (3%)
    pallas_call x1, Pallas kernels, spread_all(): pl.pallas_call(spread_kernel, out_shape=jax.ShapeDtypeStruct((devices, 2,...  31.3 us
    pallas_call x1, Pallas kernels, top(): pl.pallas_call(functools.partial(top_kernel, vec_count, pad), out_shape=(...  26.9 us
    all_to_all x1, waiting for transfers between devices, shards(): lax.all_to_all(sent, ('rep', 'shard'), split_axis=0, concat_axis=0, tiled...  24.3 us
    pallas_call x1, Pallas kernels, fold_exchange(): pl.pallas_call(fold_kernel, out_shape=jax.ShapeDtypeStruct((copies * grou...  23.9 us
    pallas_call x1, Pallas kernels, scatter(): pl.pallas_call(scatter_kernel, out_shape=jax.ShapeDtypeStruct(table.shape...  22.9 us
    pallas_call x1, Pallas kernels, forward(): pl.pallas_call(forward_kernel, out_shape=(jax.ShapeDtypeStruct(pooled.sha...  22.5 us
    pallas_call x1, Pallas kernels, pool(): pl.pallas_call(pool_kernel, out_shape=(jax.ShapeDtypeStruct((owners, ends...  14.8 us
    unnamed x6, local copies, waits for them, and re-layouts  6.58 us
  transfers between devices with their start and end apart: 1, of which 1 were waited for; matrix products, arithmetic and copies ran while one was open for 1% of the time, Pallas kernels for 12%

commit v1 on v0

v1 whole, which is shorter than its diff:
```python
import functools

import jax
import jax.numpy as jnp
from jax import lax
from jax.experimental import pallas as pl
from jax.experimental.pallas import tpu as pltpu
from jax.sharding import PartitionSpec as P

step_size = 32.0
LANES = 128
VMEM_LIMIT = 60 * 1024 * 1024
f32 = jnp.float32
bf16 = jnp.bfloat16


def whole(space):
    return pl.BlockSpec(memory_space=space)


def iota(shape, axis):
    return lax.broadcasted_iota(jnp.int32, shape, axis)


def members_of(ends, slots):
    span = ends.shape[-1]
    starts = jnp.where(iota((1, span), 1) == 0, 0, pltpu.roll(ends, 1, 1))
    places = iota((slots, span), 0)
    return ((places >= starts) & (places < ends)).astype(f32).astype(bf16)


def pool_kernel(
    first_ref, rows_ref, count_ref, ends_ref, table_ref, ids_ref, out_ref, by_sample, wide, picked,
):
    by_sample[...] = jnp.transpose(ids_ref[...])
    slots = rows_ref.shape[1]
    owners = out_ref.shape[0]
    last = count_ref.shape[1] - 1
    first = first_ref[0]
    wide[...] = table_ref[...].astype(f32)
    picked[...] = jnp.zeros_like(picked)

    def owner(o, carry):
        d = o + first

        def group(g, c):
            base = pl.multiple_of(g * 8, 8)
            parts = [wide[pl.ds(rows_ref[d, base + u], 1), :] for u in range(8)]
            picked[pl.ds(pl.multiple_of(o * slots + base, 8), 8), :] = jnp.concatenate(parts, axis=0)
            return c

        return lax.fori_loop(0, (count_ref[d, last] + 7) // 8, group, carry)

    lax.fori_loop(0, owners, owner, 0)

    def sums(o, carry):
        members = members_of(ends_ref[pl.ds(o + first, 1), :], slots)
        block = picked[pl.ds(pl.multiple_of(o * slots, 8), slots), :].astype(bf16)
        pooled = lax.dot_general(
            members, block, (((0,), (0,)), ((), ())), preferred_element_type=f32
        )
        out_ref[o] = pooled.astype(bf16)
        return carry

    lax.fori_loop(0, owners, sums, 0, unroll=4)


def pool(first, owners, rows, ends, table, ids):
    slots = rows.shape[1]
    width = table.shape[1]
    return pl.pallas_call(
        pool_kernel,
        out_shape=(
            jax.ShapeDtypeStruct((owners, ends.shape[1], width), bf16),
            jax.ShapeDtypeStruct((ids.shape[1], ids.shape[0]), ids.dtype),
        ),
        in_specs=[whole(pltpu.SMEM)] * 3 + [whole(pltpu.VMEM)] * 3,
        out_specs=(whole(pltpu.VMEM),) * 2,
        scratch_shapes=[
            pltpu.VMEM(table.shape, f32),
            pltpu.VMEM((owners * slots, width), f32),
        ],
        compiler_params=pltpu.CompilerParams(vmem_limit_bytes=VMEM_LIMIT),
        name="pool",
    )(first, rows, ends, ends, table, ids)


def spans_of(vec_count):
    return [(i, i * (i - 1) // 2) for i in range(1, vec_count)]


def top_kernel(
    vec_count, pad, index_ref, sizes_ref, dense_ref, labels_ref, small_ref, large_ref,
    w_ref, bias_ref, wout_ref, small_out, fold_out, vecs, gram, pairs, spread,
):
    batch, width = dense_ref.shape
    small_count = small_ref.shape[0]
    feats, bag_span = large_ref.shape[0], large_ref.shape[1]
    pair_pad = pairs.shape[1]
    pair_count = vec_count * (vec_count - 1) // 2
    scale = width ** (-0.5)
    spans = spans_of(vec_count)

    def rows_of(i):
        return pl.ds(i, batch, stride=pad)

    vecs[rows_of(0), :] = dense_ref[...].astype(f32)
    for t in range(small_count):
        vecs[rows_of(1 + t), :] = small_ref[t].astype(f32)
    sample = iota((batch, bag_span), 0)
    bag = iota((batch, bag_span), 1) * batch
    for f in range(feats):
        reach = sample * sizes_ref[f, index_ref[0]]
        hot = ((reach >= bag) & (reach < bag + batch)).astype(f32).astype(bf16)
        vecs[rows_of(1 + small_count + f), :] = jnp.dot(
            hot, large_ref[f], preferred_element_type=f32
        )
    for i in range(vec_count, pad):
        vecs[rows_of(i), :] = jnp.zeros((batch, width), f32)

    unroll = 8

    def gram_step(g, c):
        for u in range(unroll):
            at = pl.ds(pl.multiple_of((g * unroll + u) * pad, 8), pad)
            own = vecs[at, :].astype(bf16)
            gram[at, 0:pad] = lax.dot_general(
                own, own, (((1,), (1,)), ((), ())), preferred_element_type=f32
            )
        return c

    lax.fori_loop(0, batch // unroll, gram_step, 0)

    lane = iota((1, LANES), 1)
    chunk = 64
    for start in range(0, batch, chunk):
        tile = jnp.zeros((chunk, LANES), f32)
        at_tile = 0
        for i, off in spans:
            piece = gram[pl.ds(start * pad + i, chunk, stride=pad), :]
            turn = off % LANES
            if turn:
                piece = pltpu.roll(piece, turn, 1)
            low = off - at_tile * LANES
            tile = jnp.where((lane >= low) & (lane < low + i), piece, tile)
            if low + i >= LANES:
                pairs[start : start + chunk, at_tile * LANES : (at_tile + 1) * LANES] = (
                    tile * scale
                ).astype(bf16)
                at_tile += 1
                rest = low + i - LANES
                tile = jnp.where(lane < rest, piece, jnp.zeros_like(piece))
        if at_tile * LANES < pair_pad:
            pairs[start : start + chunk, at_tile * LANES : pair_pad] = (tile * scale).astype(bf16)

    block = 128
    labels_col = jnp.transpose(
        jnp.broadcast_to(labels_ref[...].astype(f32), (LANES, batch))
    )[:, 0:1]
    for start in range(0, batch, block):
        at = slice(start, start + block)
        preact = (
            jnp.dot(pairs[at, :], w_ref[0:pair_pad, :], preferred_element_type=f32)
            + jnp.dot(dense_ref[at, :], w_ref[pair_count : pair_count + width, :], preferred_element_type=f32)
            + bias_ref[...]
        )
        squash = jax.nn.sigmoid(preact)
        logits = jnp.sum(preact * squash * wout_ref[...], axis=1, keepdims=True)
        grad = jax.nn.sigmoid(logits) - labels_col[at, :]
        pre_grad = (
            grad * wout_ref[...] * (squash * (1.0 + preact * (1.0 - squash)))
        ).astype(bf16)
        for q in range(0, pair_pad, LANES):
            spread[at, q : q + LANES] = lax.dot_general(
                pre_grad, w_ref[q : q + LANES, :], (((1,), (1,)), ((), ())),
                preferred_element_type=f32,
            ) * scale

    gram[rows_of(0), :] = jnp.zeros((batch, LANES), f32)
    for i in range(vec_count, pad):
        gram[rows_of(i), :] = jnp.zeros((batch, LANES), f32)
    for start in range(0, batch, chunk):
        for i, off in spans:
            first = off // LANES
            low = off - first * LANES
            here = spread[start : start + chunk, first * LANES : (first + 1) * LANES]
            if low + i > LANES:
                after = spread[start : start + chunk, (first + 1) * LANES : (first + 2) * LANES]
                here = jnp.where(lane >= low, here, after)
            if low:
                here = pltpu.roll(here, LANES - low, 1)
            gram[pl.ds(start * pad + i, chunk, stride=pad), :] = jnp.where(lane < i, here, 0.0)

    def back_step(g, c):
        for u in range(unroll):
            at = pl.ds(pl.multiple_of((g * unroll + u) * pad, 8), pad)
            lower = gram[at, :]
            both = lower[:, 0:pad] + jnp.transpose(lower)[0:pad, :]
            vecs[at, :] = jnp.dot(
                both.astype(bf16), vecs[at, :].astype(bf16), preferred_element_type=f32
            )
        return c

    lax.fori_loop(0, batch // unroll, back_step, 0)

    for t in range(small_count):
        small_out[t] = vecs[rows_of(1 + t), :].astype(bf16)
    sample_lane = iota((bag_span, batch), 1)
    bag_row = iota((bag_span, batch), 0) * batch
    for f in range(feats):
        reach = sample_lane * sizes_ref[f, index_ref[0]]
        hot = ((reach >= bag_row) & (reach < bag_row + batch)).astype(f32).astype(bf16)
        fold_out[f] = jnp.dot(
            hot, vecs[rows_of(1 + small_count + f), :].astype(bf16), preferred_element_type=f32
        ).astype(bf16)


def top(index, sizes, dense, labels, small, large, w_first, bias, wout):
    batch, width = dense.shape
    small_count, feats, bag_span = small.shape[0], large.shape[0], large.shape[1]
    vec_count = 1 + small_count + feats
    pad = -(-vec_count // 8) * 8
    pair_count = vec_count * (vec_count - 1) // 2
    pair_pad = -(-pair_count // LANES) * LANES
    return pl.pallas_call(
        functools.partial(top_kernel, vec_count, pad),
        out_shape=(
            jax.ShapeDtypeStruct((small_count, batch, width), bf16),
            jax.ShapeDtypeStruct((feats, bag_span, width), bf16),
        ),
        in_specs=[whole(pltpu.SMEM)] * 2 + [whole(pltpu.VMEM)] * 7,
        out_specs=(whole(pltpu.VMEM), whole(pltpu.VMEM)),
        scratch_shapes=[
            pltpu.VMEM((batch * pad, width), f32),
            pltpu.VMEM((batch * pad, LANES), f32),
            pltpu.VMEM((batch, pair_pad), bf16),
            pltpu.VMEM((batch, pair_pad), f32),
        ],
        compiler_params=pltpu.CompilerParams(vmem_limit_bytes=VMEM_LIMIT),
        name="top",
    )(
        index, sizes, dense, labels[None, :], small, large, w_first,
        bias[None, :], wout[None, :],
    )


def greet_all():
    copies, groups = lax.axis_size("rep"), lax.axis_size("shard")
    devices = copies * groups
    index = lax.axis_index("rep") * groups + lax.axis_index("shard")
    barrier = pltpu.get_barrier_semaphore()

    def greet(k, c):
        other = lax.rem(index + k, devices)
        pl.semaphore_signal(
            barrier, inc=1, device_id={"rep": other // groups, "shard": lax.rem(other, groups)},
            device_id_type=pl.DeviceIdType.MESH,
        )
        return c

    lax.fori_loop(1, devices, greet, 0)
    pl.semaphore_wait(barrier, devices - 1)


def remote(src, dst, send, recv, rep, shard):
    return pltpu.make_async_remote_copy(
        src_ref=src, dst_ref=dst, send_sem=send, recv_sem=recv,
        device_id={"rep": rep, "shard": shard}, device_id_type=pl.DeviceIdType.MESH,
    )


def forward_kernel(pooled_ref, own_ids_ref, tables_ref, large_out, small_out, send, recv, own, tables):
    groups = lax.axis_size("shard")
    rep, me = lax.axis_index("rep"), lax.axis_index("shard")

    def block(k):
        to = lax.rem(me + k, groups)
        return remote(pooled_ref.at[to], large_out.at[me], send.at[k], recv.at[k], rep, to)

    def block_in(k):
        at = lax.rem(me + groups - k, groups)
        return remote(pooled_ref.at[at], large_out.at[at], send.at[k], recv.at[k], rep, at)

    def run(low, high, act):
        def body(k, c):
            act(k)
            return c

        lax.fori_loop(low, high, body, 0)

    fetch = pltpu.make_async_copy(tables_ref, tables, own.at[1])
    fetch.start()
    greet_all()
    run(1, groups, lambda k: block(k).start())
    mine = pltpu.make_async_copy(pooled_ref.at[me], large_out.at[me], own.at[0])
    mine.start()
    batch, small_count = own_ids_ref.shape
    rows = iota((batch, tables_ref.shape[1]), 1)
    fetch.wait()
    for t in range(small_count):
        hot = (own_ids_ref[:, t : t + 1] == rows).astype(f32).astype(bf16)
        small_out[t] = jnp.dot(hot, tables[t], preferred_element_type=f32).astype(bf16)
    mine.wait()
    run(1, groups, lambda k: block_in(k).wait_recv())
    run(1, groups, lambda k: block(k).wait_send())


def forward(pooled, own_ids, tables):
    groups = pooled.shape[0]
    return pl.pallas_call(
        forward_kernel,
        out_shape=(
            jax.ShapeDtypeStruct(pooled.shape, pooled.dtype),
            jax.ShapeDtypeStruct(
                (tables.shape[0], own_ids.shape[0], tables.shape[2]), tables.dtype
            ),
        ),
        in_specs=[whole(pltpu.VMEM)] * 2 + [whole(pl.ANY)],
        out_specs=(whole(pltpu.VMEM),) * 2,
        scratch_shapes=[pltpu.SemaphoreType.DMA((groups,))] * 2
        + [pltpu.SemaphoreType.DMA((2,)), pltpu.VMEM(tables.shape, tables.dtype)],
        compiler_params=pltpu.CompilerParams(
            collective_id=0, has_side_effects=True, vmem_limit_bytes=VMEM_LIMIT
        ),
        name="forward",
    )(pooled, own_ids, tables)


def tail_kernel(
    ids_ref, grads_ref, fold_ref, rows_ref, ends_ref, table_ref, tables_ref, small_out, large_out,
    peer_ids, peer_grads, folds, acc, lhs, rhs, keep, sent, came, sent_2, came_2, sent_3, came_3,
    prior, local, peer_s, peer_r, fold_s, fold_r, far_s, far_r, rs1_s, rs1_r, rs2_s, rs2_r,
    rs3_s, rs3_r, ag_z, ag_1, ag_2, ag_core, ag_r,
):
    groups = lax.axis_size("shard")
    ring = groups // 4
    rep, me = lax.axis_index("rep"), lax.axis_index("shard")
    z, y, core = me // 4, lax.rem(me, 4) // 2, lax.rem(me, 2)
    other = 1 - rep
    small_count, batch = ids_ref.shape
    half_count = small_count // 2
    per_unit = small_count // 16
    small_rows = keep.shape[2] // per_unit
    part = small_out.shape[5]
    slots = rows_ref.shape[1]
    spots = acc.shape[0]
    width = table_ref.shape[1]
    blocks = acc.shape[1] // width

    def shard_of(z_at, y_at, core_at):
        return z_at * 4 + y_at * 2 + core_at

    def loop(low, high, act):
        def body(k, c):
            act(k)
            return c

        lax.fori_loop(low, high, body, 0)

    peer = shard_of(z, y, 1 - core)
    away = (1 - core) * half_count
    swap = [
        remote(ids_ref.at[pl.ds(pl.multiple_of(away, 8), half_count)], peer_ids, peer_s.at[0], peer_r.at[0], rep, peer),
        remote(grads_ref.at[pl.ds(away, half_count)], peer_grads, peer_s.at[1], peer_r.at[1], rep, peer),
    ]

    def out_block(k):
        to = lax.rem(me + k, groups)
        return remote(fold_ref.at[to], folds.at[rep * groups + me], fold_s.at[k], fold_r.at[k], rep, to)

    def in_block(k):
        at = lax.rem(me + groups - k, groups)
        return remote(fold_ref.at[at], folds.at[rep * groups + at], fold_s.at[k], fold_r.at[k], rep, at)

    def far_out(k):
        slot = folds.at[rep * groups + lax.rem(me + groups - k, groups)]
        return remote(slot, slot, far_s.at[k], far_r.at[k], other, me)

    def far_in(k):
        slot = folds.at[other * groups + lax.rem(me + groups - k, groups)]
        return remote(slot, slot, far_s.at[k], far_r.at[k], other, me)

    own_far = remote(fold_ref.at[me], folds.at[rep * groups + me], far_s.at[0], far_r.at[0], other, me)

    greet_all()
    for copy in swap:
        copy.start()
    loop(1, groups, lambda k: out_block(k).start())
    own_far.start()
    fetch = [
        pltpu.make_async_copy(tables_ref.at[core, h, rep, y, z], prior.at[h], local.at[h])
        for h in range(2)
    ]
    for copy in fetch:
        copy.start()
    folds[rep * groups + me] = fold_ref[me]
    acc[...] = jnp.zeros_like(acc)
    for copy in swap:
        copy.wait_recv()

    row = iota((small_rows, batch), 0)

    def dense(t):
        own = (row == ids_ref[pl.ds(core * half_count + t, 1), :]).astype(f32).astype(bf16)
        far = (row == peer_ids[pl.ds(t, 1), :]).astype(f32).astype(bf16)
        return jnp.dot(
            own, grads_ref[core * half_count + t], preferred_element_type=f32
        ) + jnp.dot(far, peer_grads[t], preferred_element_type=f32)

    def first_hop(h, s):
        to_rep = rep + (1 - h) * (1 - 2 * rep)
        to_y = y + h * (1 - 2 * y)
        return remote(
            sent.at[h, s], came.at[h, s], rs1_s.at[h, s], rs1_r.at[h, s], to_rep, shard_of(z, to_y, core)
        )

    def second_hop(h):
        to_rep = rep + h * (1 - 2 * rep)
        to_y = y + (1 - h) * (1 - 2 * y)
        return remote(
            sent_2.at[h], came_2.at[h], rs2_s.at[h], rs2_r.at[h], to_rep, shard_of(z, to_y, core)
        )

    def third_hop(h, k):
        to = lax.rem(z + k, ring)
        return remote(
            sent_3.at[h, to], came_3.at[h, z], rs3_s.at[h, k], rs3_r.at[h, k], rep, shard_of(to, y, core)
        )

    def third_in(h, k):
        at = lax.rem(z + ring - k, ring)
        return remote(
            sent_3.at[h, at], came_3.at[h, at], rs3_s.at[h, k], rs3_r.at[h, k], rep, shard_of(at, y, core)
        )

    def give(i):
        s, h = i // 2, lax.rem(i, 2)
        r_at = other + h * s * (2 * rep - 1)
        y_at = (1 - y) + (1 - h) * s * (2 * y - 1)
        first = ((h * 2 + r_at) * 2 + y_at) * per_unit
        for j in range(per_unit):
            sent[h, s, j * small_rows : (j + 1) * small_rows, :] = dense(first + j).astype(bf16)
        first_hop(h, s).start()

    def hold(i):
        s, h = i // 2, lax.rem(i, 2)
        r_at = rep + h * (1 - s) * (1 - 2 * rep)
        y_at = y + (1 - h) * (1 - s) * (1 - 2 * y)
        first = ((h * 2 + r_at) * 2 + y_at) * per_unit
        for j in range(per_unit):
            keep[h, s, j * small_rows : (j + 1) * small_rows, :] = dense(first + j)

    loop(0, 4, give)
    loop(0, 4, hold)

    spot = iota((spots, slots), 0)

    def spread_one(d, v):
        members = members_of(ends_ref[pl.ds(d, 1), :], slots)
        moved = jnp.dot(members, folds[d], preferred_element_type=f32)
        at = rows_ref[pl.ds(d, 1), :]
        block = at // spots
        wide = jnp.transpose(jnp.broadcast_to(block.astype(f32), (width, slots)))
        for q in range(blocks):
            rhs[v * slots : (v + 1) * slots, q * width : (q + 1) * width] = jnp.where(
                wide == q, moved, 0.0
            ).astype(bf16)
        lhs[:, v * slots : (v + 1) * slots] = (spot == at - block * spots).astype(f32).astype(bf16)

    step = 2 * width

    def spread_pair(d, e):
        spread_one(d, 0)
        spread_one(e, 1)

        def add(n):
            at = pl.ds(pl.multiple_of(n * step, step), step)
            acc[:, at] += jnp.dot(lhs[...], rhs[:, at], preferred_element_type=f32)

        loop(0, acc.shape[1] // step, add)

    def take(k):
        in_block(k).wait_recv()
        far_out(k).start()

    def near(k):
        return rep * groups + lax.rem(me + groups - k, groups)

    def near_pair(p):
        @pl.when(p > 0)
        def _():
            take(2 * p)

        take(2 * p + 1)
        spread_pair(near(2 * p), near(2 * p + 1))

    def far_pair(p):
        far_in(2 * p).wait_recv()
        far_in(2 * p + 1).wait_recv()
        spread_pair(
            other * groups + lax.rem(me + groups - 2 * p, groups),
            other * groups + lax.rem(me + groups - 2 * p - 1, groups),
        )

    pairs = groups // 2
    cut_1, cut_2 = pairs * 3 // 8, pairs // 2
    loop(0, cut_1, near_pair)

    def turn(h):
        first_hop(h, 0).wait_recv()
        sent_2[h] = (keep[h, 0] + came[h, 0].astype(f32)).astype(bf16)
        second_hop(h).start()

    loop(0, 2, turn)
    loop(cut_1, pairs, near_pair)

    def along(h):
        first_hop(h, 1).wait_recv()
        second_hop(h).wait_recv()
        total = keep[h, 1] + came[h, 1].astype(f32) + came_2[h].astype(f32)
        keep[h, 1] = total
        sent_3[h] = total.astype(bf16).reshape(ring, part, width)
        loop(1, ring, lambda k: third_hop(h, k).start())

    loop(0, 2, along)
    loop(0, cut_2, far_pair)

    for copy in fetch:
        copy.wait()

    def own_part(h):
        total = keep[h, 1, pl.ds(pl.multiple_of(z * part, part), part), :]
        for k in range(1, ring):
            third_in(h, k).wait_recv()
            total = total + came_3[h, lax.rem(z + ring - k, ring)].astype(f32)
        small_out[core, h, rep, y, z] = (prior[h].astype(f32) - step_size * total).astype(bf16)

    loop(0, 2, own_part)

    pending = []

    def place(h, rep_at, z_at, y_at, core_at):
        return small_out.at[core_at, h, rep_at, y_at, z_at]

    def slot_of(rep_at, z_at, y_at, core_at):
        return rep_at * groups + shard_of(z_at, y_at, core_at)

    def send(h, rep_at, z_at, y_at, sem, to_rep, to_z, to_y, to_core):
        block = place(h, rep_at, z_at, y_at, core)
        copy = remote(
            block, block, sem, ag_r.at[h, slot_of(rep_at, z_at, y_at, core)],
            to_rep, shard_of(to_z, to_y, to_core),
        )
        copy.start()
        pending.append(copy)

    def arrived(h, rep_at, z_at, y_at, core_at):
        block = place(h, rep_at, z_at, y_at, core_at)
        remote(
            block, block, local.at[2], ag_r.at[h, slot_of(rep_at, z_at, y_at, core_at)], rep, peer
        ).wait_recv()

    def second(h, k, rep_at, z_at, y_at):
        hop = (rep, z, 1 - y, core) if h == 0 else (other, z, y, core)
        send(h, rep_at, z_at, y_at, ag_1.at[h, k], *hop)

    def third(h, k, rep_at, z_at, y_at):
        hop = (other, z, y, core) if h == 0 else (rep, z, 1 - y, core)
        send(h, rep_at, z_at, y_at, ag_2.at[h, k], *hop)

    def last(h, k, rep_at, z_at, y_at):
        send(h, rep_at, z_at, y_at, ag_core.at[h, k], rep, z, y, 1 - core)

    for k in range(1, ring):
        for h in range(2):
            send(h, rep, z, y, ag_z.at[h, k], rep, lax.rem(z + k, ring), y, core)
    for h in range(2):
        second(h, 0, rep, z, y)
        third(h, 0, rep, z, y)
        last(h, 0, rep, z, y)

    loop(cut_2, pairs, far_pair)
    for q in range(blocks):
        at = slice(q * spots, (q + 1) * spots)
        large_out[at, :] = (
            table_ref[at, :].astype(f32) - step_size * acc[:, q * width : (q + 1) * width]
        ).astype(bf16)

    for k in range(1, ring):
        z_at = lax.rem(z + ring - k, ring)
        for h in range(2):
            arrived(h, rep, z_at, y, core)
            second(h, k, rep, z_at, y)
            third(h, k, rep, z_at, y)
            last(h, k, rep, z_at, y)
    for k in range(ring):
        z_at = lax.rem(z + ring - k, ring)
        for h in range(2):
            where = (rep, z_at, 1 - y) if h == 0 else (other, z_at, y)
            arrived(h, *where, core)
            third(h, ring + k, *where)
            last(h, ring + k, *where)
    for k in range(2 * ring):
        z_at = lax.rem(z + ring - k % ring, ring)
        for h in range(2):
            if h == 0:
                where = (other, z_at, y if k < ring else 1 - y)
            else:
                where = (rep if k < ring else other, z_at, 1 - y)
            arrived(h, *where, core)
            last(h, 2 * ring + k, *where)
    for r in range(2):
        for k in range(ring):
            for y_at in range(2):
                for h in range(2):
                    arrived(h, r, k, y_at, 1 - core)

    for copy in pending + swap:
        copy.wait_send()
    own_far.wait_send()
    loop(1, groups, lambda k: out_block(k).wait_send())
    loop(1, groups, lambda k: far_out(k).wait_send())
    loop(0, 4, lambda i: first_hop(lax.rem(i, 2), i // 2).wait_send())
    loop(0, 2, lambda h: second_hop(h).wait_send())
    for h in range(2):
        loop(1, ring, lambda k: third_hop(h, k).wait_send())


def tail(ids, grads, fold, rows, ends, table, tables):
    groups = fold.shape[0]
    devices, slots = rows.shape
    ring = groups // 4
    small_count, small_rows, width = tables.shape
    part = small_count * small_rows // devices // 2
    unit = small_count * small_rows // 16
    blocks = 8
    split = (2, 2, 2, 2, ring, part, width)
    dma = pltpu.SemaphoreType.DMA
    small, large = pl.pallas_call(
        tail_kernel,
        out_shape=(
            jax.ShapeDtypeStruct(split, bf16),
            jax.ShapeDtypeStruct(table.shape, bf16),
        ),
        in_specs=[whole(pltpu.VMEM)] * 6 + [whole(pl.ANY)],
        out_specs=(whole(pltpu.VMEM),) * 2,
        scratch_shapes=[
            pltpu.VMEM((small_count // 2, ids.shape[1]), ids.dtype),
            pltpu.VMEM((small_count // 2,) + grads.shape[1:], bf16),
            pltpu.VMEM((devices,) + fold.shape[1:], bf16),
            pltpu.VMEM((table.shape[0] // blocks, blocks * width), f32),
            pltpu.VMEM((table.shape[0] // blocks, 2 * slots), bf16),
            pltpu.VMEM((2 * slots, blocks * width), bf16),
            pltpu.VMEM((2, 2, unit, width), f32),
            pltpu.VMEM((2, 2, unit, width), bf16),
            pltpu.VMEM((2, 2, unit, width), bf16),
            pltpu.VMEM((2, unit, width), bf16),
            pltpu.VMEM((2, unit, width), bf16),
            pltpu.VMEM((2, ring, part, width), bf16),
            pltpu.VMEM((2, ring, part, width), bf16),
            pltpu.VMEM((2, part, width), bf16),
            dma((3,)), dma((2,)), dma((2,)),
            dma((groups,)), dma((groups,)), dma((groups,)), dma((groups,)),
            dma((2, 2)), dma((2, 2)), dma((2,)), dma((2,)), dma((2, ring)), dma((2, ring)),
            dma((2, ring)), dma((2, ring)), dma((2, 2 * ring)), dma((2, 4 * ring)), dma((2, devices)),
        ],
        compiler_params=pltpu.CompilerParams(
            collective_id=1, has_side_effects=True, vmem_limit_bytes=VMEM_LIMIT
        ),
        name="tail",
    )(ids, grads, fold, rows, ends, table, tables.reshape(split))
    return small.reshape(tables.shape), large


def store_kernel(small_ref, large_ref, small_out, large_out, sems):
    pieces = 4
    copies = []
    for n, (src, dst) in enumerate(((small_ref, small_out), (large_ref, large_out))):
        size = src.shape[0] // pieces
        for p in range(pieces):
            at = pl.ds(p * size, size)
            copies.append(pltpu.make_async_copy(src.at[at], dst.at[at], sems.at[n, p]))
    for copy in copies:
        copy.start()
    for copy in copies:
        copy.wait()


def store(small, large):
    return pl.pallas_call(
        store_kernel,
        out_shape=(
            jax.ShapeDtypeStruct(small.shape, small.dtype),
            jax.ShapeDtypeStruct(large.shape, large.dtype),
        ),
        in_specs=[whole(pltpu.VMEM)] * 2,
        out_specs=(whole(pl.ANY),) * 2,
        scratch_shapes=[pltpu.SemaphoreType.DMA((2, 4))],
        compiler_params=pltpu.CompilerParams(vmem_limit_bytes=16 * 1024 * 1024),
        name="store",
    )(small, large)


def shards(
    dense, small_ids, labels, small_tables, large_tables, batch_sizes, bag_ends,
    owner_row_index, w_first, b_first, w_out,
):
    groups = lax.axis_size("shard")
    first = lax.axis_index("rep") * groups
    index = first + lax.axis_index("shard")
    ends, rows, table = bag_ends[0], owner_row_index[0], large_tables[0]
    ids = jnp.transpose(small_ids)

    pooled, own_ids = pool(first[None], groups, rows, ends, table, ids)
    large, small = forward(pooled, own_ids, small_tables)
    small_grads, fold = top(
        index[None], batch_sizes, dense, labels, small, large, w_first, b_first, w_out
    )
    small_new, large_new = tail(ids, small_grads, fold, rows, ends, table, small_tables)
    small_new, large_new = store(small_new, large_new)
    return small_new, large_new[None]


def solution(mesh):
    both = ("rep", "shard")
    placed = (
        P(both, None), P(both, None), P(both), P(), P("shard", None, None), P(),
        P("shard", None, None), P("shard", None, None), P(), P(), P(),
    )
    return jax.shard_map(
        shards, mesh=mesh, in_specs=placed, out_specs=(P(), P("shard", None, None)), check_vma=False
    )
```

time: 188 us -> 147 us (0.78)
  waiting for transfers between devices: 24.3 us -> 0 us
  starting transfers between devices: 6.32 us -> 0 us
  Pallas kernels: 147 us -> 142 us
  local copies, waits for them, and re-layouts: 8.14 us -> 3.77 us
    all_to_all x1 -> x0, waiting for transfers between devices: 24.3 us -> none  [shards(): lax.all_to_all(sent, ('rep', 'shard'), split_axis=0, concat_axis=0, tiled...]
    all_to_all x1 -> x0, starting transfers between devices: 6.32 us -> none  [shards(): lax.all_to_all(sent, ('rep', 'shard'), split_axis=0, concat_axis=0, tiled...]
    pallas_call x1, Pallas kernels: 14.8 us -> 11.9 us  [pool(): pl.pallas_call(pool_kernel, out_shape=(jax.ShapeDtypeStruct((owners, ends...]
    unnamed x6 -> x4, local copies, waits for them, and re-layouts: 6.58 us -> 3.77 us
    pallas_call x1, Pallas kernels: 22.5 us -> 19.9 us  [forward(): pl.pallas_call(forward_kernel, out_shape=(jax.ShapeDtypeStruct(pooled.sha...]
    pallas_call x4 -> x2, Pallas kernels: 83.2 us -> 82.9 us  [the longest x1 80.2 us: tail(): pl.pallas_call(tail_kernel, out_shape=(jax.ShapeDtypeStruct(split, bf16),...]
  transfers between devices with their start and end apart: 1 -> 0, of which waited for: 1 -> 0; matrix products, arithmetic and copies ran while one was open for 1% -> 0% of each run, Pallas kernels for 12% -> 0%
where the time goes in v1:
time: 147 us; the launch traced here: 146 us
  Pallas kernels  142 us (97%)
  local copies, waits for them, and re-layouts  3.77 us (3%)
    pallas_call x1, Pallas kernels, tail(): pl.pallas_call(tail_kernel, out_shape=(jax.ShapeDtypeStruct(split, bf16),...  80.2 us
    pallas_call x1, Pallas kernels, top(): pl.pallas_call(functools.partial(top_kernel, vec_count, pad), out_shape=(...  26.9 us
    pallas_call x1, Pallas kernels, forward(): pl.pallas_call(forward_kernel, out_shape=(jax.ShapeDtypeStruct(pooled.sha...  19.9 us
    pallas_call x1, Pallas kernels, pool(): pl.pallas_call(pool_kernel, out_shape=(jax.ShapeDtypeStruct((owners, ends...  11.9 us
    unnamed x4, local copies, waits for them, and re-layouts  3.77 us

profile of v1, /device:TPU:1, one launch (start us, length us, event | category | flops | bytes accessed | tf_op | source)
XLA Modules:
  0.0 146.2 jit_solution(15051489750197506785)
XLA Ops:
  0.6 11.9 %pool.1 = (bf16[16,128,128]{2,1,0:T(8,128)(2,1)}, s32[256,32]{1,0:T(8,128)}) custom-call(s32[1]{0:T(128)} %bitcast.3.first_ref, s32[32,256]{1,0:T(8,128)} %bitcast.21, s32[32,128]{1,0:T(8,128)} %bitcast.16, s32[32,128]{1,0:T(8,128)} %bitcast.17, bf16[8192,128]{1,0:T(8,128)(2,1)} %bitcast.14, s32[32,256]{1,0:T(8,128)} %bitcast.19), custom_call_target="tpu_custom_call" | custom-call | tf_op jit(solution)/shard_map/pool/pallas_call | solution.py:71
  12.5 19.9 %forward.1 = (bf16[16,128,128]{2,1,0:T(8,128)(2,1)}, bf16[32,256,128]{2,1,0:T(8,128)(2,1)}) custom-call(bf16[16,128,128]{2,1,0:T(8,128)(2,1)} %get-tuple-element.12.pooled_ref, s32[256,32]{1,0:T(8,128)} %get-tuple-element.13.own_ids_ref, bf16[32,512,128]{2,1,0:T(8,128)(2,1)} %tables_ref.1), custom_call_target="tpu_custom_call" | custom-call | tf_op jit(solution)/shard_map/forward/pallas_call | solution.py:310
  32.4 26.9 %top.1 = (bf16[32,256,128]{2,1,0:T(8,128)(2,1)}, bf16[16,128,128]{2,1,0:T(8,128)(2,1)}) custom-call(s32[1]{0:T(128)} %bitcast.1.index_ref, s32[16,32]{1,0:T(8,128)} %sizes_ref.1, bf16[256,128]{1,0:T(8,128)(2,1)} %dense_ref.1, s32[1,256]{1,0:T(1,128)} %bitcast.25, bf16[32,256,128]{2,1,0:T(8,128)(2,1)} %get-tuple-element.14.small_ref, ...), custom_call_target="tpu_custom_call" | custom-call | tf_op jit(solution)/shard_map/top/pallas_call | solution.py:225
  59.3 80.2 %tail.1 = (bf16[2,2,2,2,4,256,128]{6,5,4,3,2,1,0:T(8,128)(2,1)}, bf16[8192,128]{1,0:T(8,128)(2,1)}) custom-call(s32[32,256]{1,0:T(8,128)} %bitcast.20, bf16[32,256,128]{2,1,0:T(8,128)(2,1)} %get-tuple-element.16.grads_ref, bf16[16,128,128]{2,1,0:T(8,128)(2,1)} %get-tuple-element.17.fold_ref, s32[32,256]{1,0:T(8,128)} %bitcast.22, s32[32,128]{1,0:T(8,128)} %bitcast.18, ...), custom_call_target="tpu_custom_call" | custom-call | tf_op jit(solution)/shard_map/tail/pallas_call | solution.py:639
  139.5 0.0 copy-start
  139.5 2.2 %copy-done = bf16[2,2,2,2,4,256,128]{6,5,4,3,2,1,0:T(8,128)(2,1)S(1)} copy-done((bf16[2,2,2,2,4,256,128]{6,5,4,3,2,1,0:T(8,128)(2,1)S(1)}, bf16[2,2,2,2,4,256,128]{6,5,4,3,2,1,0:T(8,128)(2,1)}, u32[]{:S(2)}) %copy-start) | copy-done | bytes 4194328
  141.7 0.0 copy-start.1
  141.7 1.6 %copy-done.1 = bf16[8192,128]{1,0:T(8,128)(2,1)S(1)} copy-done((bf16[8192,128]{1,0:T(8,128)(2,1)S(1)}, bf16[8192,128]{1,0:T(8,128)(2,1)}, u32[]{:S(2)}) %copy-start.1) | copy-done | bytes 2097176
  143.3 2.7 %store.1 = (bf16[32,512,128]{2,1,0:T(8,128)(2,1)}, bf16[8192,128]{1,0:T(8,128)(2,1)}) custom-call(bf16[32,512,128]{2,1,0:T(8,128)(2,1)S(1)} %bitcast.12, bf16[8192,128]{1,0:T(8,128)(2,1)S(1)} %copy-done.1), custom_call_target="tpu_custom_call" | custom-call | tf_op jit(solution)/shard_map/store/pallas_call | solution.py:690
Async XLA Ops:
  139.5 2.2 %copy-start = (bf16[2,2,2,2,4,256,128]{6,5,4,3,2,1,0:T(8,128)(2,1)S(1)}, bf16[2,2,2,2,4,256,128]{6,5,4,3,2,1,0:T(8,128)(2,1)}, u32[]{:S(2)}) copy-start(bf16[2,2,2,2,4,256,128]{6,5,4,3,2,1,0:T(8,128)(2,1)} %get-tuple-element.18) | copy-start | bytes 12582916
  141.7 1.6 %copy-start.1 = (bf16[8192,128]{1,0:T(8,128)(2,1)S(1)}, bf16[8192,128]{1,0:T(8,128)(2,1)}, u32[]{:S(2)}) copy-start(bf16[8192,128]{1,0:T(8,128)(2,1)} %get-tuple-element.19.large_ref) | copy-start | bytes 6291460

commit v2 on v1

--- a/solution.py
+++ b/solution.py
@@ -1,4 +1,5 @@
 import functools
+import math
 
 import jax
 import jax.numpy as jnp
@@ -10,12 +11,18 @@
 step_size = 32.0
 LANES = 128
 VMEM_LIMIT = 60 * 1024 * 1024
+MIB = 1024 * 1024
 f32 = jnp.float32
 bf16 = jnp.bfloat16
 
 
 def whole(space):
     return pl.BlockSpec(memory_space=space)
+
+
+def grant(*arrays):
+    total = sum(math.prod(a.shape) * jnp.dtype(a.dtype).itemsize for a in arrays)
+    return min(VMEM_LIMIT, total + 6 * MIB)
 
 
 def iota(shape, axis):
@@ -68,6 +75,7 @@
 def pool(first, owners, rows, ends, table, ids):
     slots = rows.shape[1]
     width = table.shape[1]
+    scratch = [pltpu.VMEM(table.shape, f32), pltpu.VMEM((owners * slots, width), f32)]
     return pl.pallas_call(
         pool_kernel,
         out_shape=(
@@ -76,11 +84,8 @@
         ),
         in_specs=[whole(pltpu.SMEM)] * 3 + [whole(pltpu.VMEM)] * 3,
         out_specs=(whole(pltpu.VMEM),) * 2,
-        scratch_shapes=[
-            pltpu.VMEM(table.shape, f32),
-            pltpu.VMEM((owners * slots, width), f32),
-        ],
-        compiler_params=pltpu.CompilerParams(vmem_limit_bytes=VMEM_LIMIT),
+        scratch_shapes=scratch,
+        compiler_params=pltpu.CompilerParams(vmem_limit_bytes=grant(table, ids, ids, ends, *scratch)),
         name="pool",
     )(first, rows, ends, ends, table, ids)
 
@@ -222,6 +227,12 @@
     pad = -(-vec_count // 8) * 8
     pair_count = vec_count * (vec_count - 1) // 2
     pair_pad = -(-pair_count // LANES) * LANES
+    scratch = [
+        pltpu.VMEM((batch * pad, width), f32),
+        pltpu.VMEM((batch * pad, LANES), f32),
+        pltpu.VMEM((batch, pair_pad), bf16),
+        pltpu.VMEM((batch, pair_pad), f32),
+    ]
     return pl.pallas_call(
         functools.partial(top_kernel, vec_count, pad),
         out_shape=(
@@ -230,13 +241,10 @@
         ),
         in_specs=[whole(pltpu.SMEM)] * 2 + [whole(pltpu.VMEM)] * 7,
         out_specs=(whole(pltpu.VMEM), whole(pltpu.VMEM)),
-        scratch_shapes=[
-            pltpu.VMEM((batch * pad, width), f32),
-            pltpu.VMEM((batch * pad, LANES), f32),
-            pltpu.VMEM((batch, pair_pad), bf16),
-            pltpu.VMEM((batch, pair_pad), f32),
-        ],
-        compiler_params=pltpu.CompilerParams(vmem_limit_bytes=VMEM_LIMIT),
+        scratch_shapes=scratch,
+        compiler_params=pltpu.CompilerParams(
+            vmem_limit_bytes=grant(dense, small, large, small, large, w_first, *scratch)
+        ),
         name="top",
     )(
         index, sizes, dense, labels[None, :], small, large, w_first,
@@ -307,20 +315,19 @@
 
 def forward(pooled, own_ids, tables):
     groups = pooled.shape[0]
+    small = jax.ShapeDtypeStruct(
+        (tables.shape[0], own_ids.shape[0], tables.shape[2]), tables.dtype
+    )
     return pl.pallas_call(
         forward_kernel,
-        out_shape=(
-            jax.ShapeDtypeStruct(pooled.shape, pooled.dtype),
-            jax.ShapeDtypeStruct(
-                (tables.shape[0], own_ids.shape[0], tables.shape[2]), tables.dtype
-            ),
-        ),
+        out_shape=(jax.ShapeDtypeStruct(pooled.shape, pooled.dtype), small),
         in_specs=[whole(pltpu.VMEM)] * 2 + [whole(pl.ANY)],
         out_specs=(whole(pltpu.VMEM),) * 2,
         scratch_shapes=[pltpu.SemaphoreType.DMA((groups,))] * 2
         + [pltpu.SemaphoreType.DMA((2,)), pltpu.VMEM(tables.shape, tables.dtype)],
         compiler_params=pltpu.CompilerParams(
-            collective_id=0, has_side_effects=True, vmem_limit_bytes=VMEM_LIMIT
+            collective_id=0, has_side_effects=True,
+            vmem_limit_bytes=grant(pooled, pooled, own_ids, tables, small),
         ),
         name="forward",
     )(pooled, own_ids, tables)
@@ -635,6 +642,22 @@
     unit = small_count * small_rows // 16
     blocks = 8
     split = (2, 2, 2, 2, ring, part, width)
+    scratch = [
+        pltpu.VMEM((small_count // 2, ids.shape[1]), ids.dtype),
+        pltpu.VMEM((small_count // 2,) + grads.shape[1:], bf16),
+        pltpu.VMEM((devices,) + fold.shape[1:], bf16),
+        pltpu.VMEM((table.shape[0] // blocks, blocks * width), f32),
+        pltpu.VMEM((table.shape[0] // blocks, 2 * slots), bf16),
+        pltpu.VMEM((2 * slots, blocks * width), bf16),
+        pltpu.VMEM((2, 2, unit, width), f32),
+        pltpu.VMEM((2, 2, unit, width), bf16),
+        pltpu.VMEM((2, 2, unit, width), bf16),
+        pltpu.VMEM((2, unit, width), bf16),
+        pltpu.VMEM((2, unit, width), bf16),
+        pltpu.VMEM((2, ring, part, width), bf16),
+        pltpu.VMEM((2, ring, part, width), bf16),
+        pltpu.VMEM((2, part, width), bf16),
+    ]
     dma = pltpu.SemaphoreType.DMA
     small, large = pl.pallas_call(
         tail_kernel,
@@ -644,28 +667,15 @@
         ),
         in_specs=[whole(pltpu.VMEM)] * 6 + [whole(pl.ANY)],
         out_specs=(whole(pltpu.VMEM),) * 2,
-        scratch_shapes=[
-            pltpu.VMEM((small_count // 2, ids.shape[1]), ids.dtype),
-            pltpu.VMEM((small_count // 2,) + grads.shape[1:], bf16),
-            pltpu.VMEM((devices,) + fold.shape[1:], bf16),
-            pltpu.VMEM((table.shape[0] // blocks, blocks * width), f32),
-            pltpu.VMEM((table.shape[0] // blocks, 2 * slots), bf16),
-            pltpu.VMEM((2 * slots, blocks * width), bf16),
-            pltpu.VMEM((2, 2, unit, width), f32),
-            pltpu.VMEM((2, 2, unit, width), bf16),
-            pltpu.VMEM((2, 2, unit, width), bf16),
-            pltpu.VMEM((2, unit, width), bf16),
-            pltpu.VMEM((2, unit, width), bf16),
-            pltpu.VMEM((2, ring, part, width), bf16),
-            pltpu.VMEM((2, ring, part, width), bf16),
-            pltpu.VMEM((2, part, width), bf16),
+        scratch_shapes=scratch + [
             dma((3,)), dma((2,)), dma((2,)),
             dma((groups,)), dma((groups,)), dma((groups,)), dma((groups,)),
             dma((2, 2)), dma((2, 2)), dma((2,)), dma((2,)), dma((2, ring)), dma((2, ring)),
             dma((2, ring)), dma((2, ring)), dma((2, 2 * ring)), dma((2, 4 * ring)), dma((2, devices)),
         ],
         compiler_params=pltpu.CompilerParams(
-            collective_id=1, has_side_effects=True, vmem_limit_bytes=VMEM_LIMIT
+            collective_id=1, has_side_effects=True,
+            vmem_limit_bytes=grant(ids, grads, fold, rows, ends, table, table, tables, *scratch),
         ),
         name="tail",
     )(ids, grads, fold, rows, ends, table, tables.reshape(split))

time: 147 us -> 139 us (0.946)
  Pallas kernels: 142 us -> 131 us
  local copies, waits for them, and re-layouts: 3.77 us -> 6.06 us
    pallas_call x1, Pallas kernels: 80.2 us -> 75.6 us  [tail(): pl.pallas_call(tail_kernel, out_shape=(jax.ShapeDtypeStruct(split, bf16),...]
    pallas_call x1, Pallas kernels: 26.9 us -> 23.7 us  [top(): pl.pallas_call(functools.partial(top_kernel, vec_count, pad), out_shape=(...]
    unnamed x4 -> x32, local copies, waits for them, and re-layouts: 3.77 us -> 6.06 us
    pallas_call x1, Pallas kernels: 19.9 us -> 17.7 us  [forward(): pl.pallas_call(forward_kernel, out_shape=(jax.ShapeDtypeStruct(pooled.sha...]
where the time goes in v2:
time: 139 us; the launch traced here: 138 us
  Pallas kernels  131 us (94%)
  local copies, waits for them, and re-layouts  6.06 us (4%)
    pallas_call x1, Pallas kernels, tail(): pl.pallas_call(tail_kernel, out_shape=(jax.ShapeDtypeStruct(split, bf16),...  75.6 us
    pallas_call x1, Pallas kernels, top(): pl.pallas_call(functools.partial(top_kernel, vec_count, pad), out_shape=(...  23.7 us
    pallas_call x1, Pallas kernels, forward(): pl.pallas_call(forward_kernel, out_shape=(jax.ShapeDtypeStruct(pooled.sha...  17.7 us
    pallas_call x1, Pallas kernels, pool(): pl.pallas_call(pool_kernel, out_shape=(jax.ShapeDtypeStruct((owners, ends...  11 us
    unnamed x32, local copies, waits for them, and re-layouts  6.06 us

profile of v2, /device:TPU:1, one launch (start us, length us, event | category | flops | bytes accessed | tf_op | source)
XLA Modules:
  0.0 137.9 jit_solution(16414231130462128204)
XLA Ops:
  0.6 0.0 copy-start.2
  0.6 1.6 %copy-done.2 = bf16[1,8192,128]{2,1,0:T(8,128)(2,1)S(1)} copy-done((bf16[1,8192,128]{2,1,0:T(8,128)(2,1)S(1)}, bf16[1,8192,128]{2,1,0:T(8,128)(2,1)}, u32[]{:S(2)}) %copy-start.2) | copy-done | bytes 2097176
  2.2 0.0 copy-start.5
  2.2 0.7 copy-done.5
  2.9 0.0 copy-start.7
  2.9 0.8 copy-done.7
  3.7 0.8 copy-done.9
  4.5 11.0 %pool.1 = (bf16[16,128,128]{2,1,0:T(8,128)(2,1)S(1)}, s32[256,32]{1,0:T(8,128)S(1)}) custom-call(s32[1]{0:T(128)} %bitcast.3.first_ref, s32[32,256]{1,0:T(8,128)S(1)} %bitcast.21, s32[32,128]{1,0:T(8,128)S(1)} %bitcast.16, s32[32,128]{1,0:T(8,128)S(1)} %bitcast.17, bf16[8192,128]{1,0:T(8,128)(2,1)S(1)} %bitcast.13, s32[32,256]{1,0:T(8,128)S(1)} %bitcast.19), custom_call_target="tpu_custom_call" | custom-call | tf_op jit(solution)/shard_map/pool/pallas_call | solution.py:79
  15.5 0.0 copy-start
  15.5 2.2 %copy-done = bf16[32,512,128]{2,1,0:T(8,128)(2,1)S(1)} copy-done((bf16[32,512,128]{2,1,0:T(8,128)(2,1)S(1)}, bf16[32,512,128]{2,1,0:T(8,128)(2,1)}, u32[]{:S(2)}) %copy-start) | copy-done | bytes 4194328
  17.7 0.0 copy-start.14
  17.7 0.0 copy-start.15
  17.7 0.0 copy-start.3
  17.7 17.7 %forward.1 = (bf16[16,128,128]{2,1,0:T(8,128)(2,1)S(1)}, bf16[32,256,128]{2,1,0:T(8,128)(2,1)S(1)}) custom-call(bf16[16,128,128]{2,1,0:T(8,128)(2,1)S(1)} %get-tuple-element.12.pooled_ref, s32[256,32]{1,0:T(8,128)S(1)} %get-tuple-element.13.own_ids_ref, bf16[32,512,128]{2,1,0:T(8,128)(2,1)S(1)} %copy-done), custom_call_target="tpu_custom_call" | custom-call | tf_op jit(solution)/shard_map/forward/pallas_call | solution.py:321
  35.5 0.0 copy-done.4
  35.5 0.0 copy-done.11
  35.5 0.0 copy-done.12
  35.5 0.0 copy-done.13
  35.5 0.0 copy-done.14
  35.5 0.0 copy-done.15
  35.5 0.0 copy-start.1
  35.5 0.0 copy-start.6
  35.6 0.0 copy-start.8
  35.6 0.0 copy-start.10
  35.6 23.7 %top.1 = (bf16[32,256,128]{2,1,0:T(8,128)(2,1)S(1)}, bf16[16,128,128]{2,1,0:T(8,128)(2,1)S(1)}) custom-call(s32[1]{0:T(128)} %bitcast.1.index_ref, s32[16,32]{1,0:T(8,128)S(1)} %copy-done.12, bf16[256,128]{1,0:T(8,128)(2,1)S(1)} %copy-done.11, s32[1,256]{1,0:T(1,128)S(1)} %bitcast.25, bf16[32,256,128]{2,1,0:T(8,128)(2,1)S(1)} %get-tuple-element.14.small_ref, ...), custom_call_target="tpu_custom_call" | custom-call | tf_op jit(solution)/shard_map/top/pallas_call | solution.py:236
  59.3 0.0 copy-done.3
  59.3 0.0 copy-done.1
  59.3 0.0 copy-done.6
  59.3 0.0 copy-done.8
  59.3 0.0 copy-done.10
  59.3 75.6 %tail.1 = (bf16[2,2,2,2,4,256,128]{6,5,4,3,2,1,0:T(8,128)(2,1)S(1)}, bf16[8192,128]{1,0:T(8,128)(2,1)S(1)}) custom-call(s32[32,256]{1,0:T(8,128)S(1)} %bitcast.20, bf16[32,256,128]{2,1,0:T(8,128)(2,1)S(1)} %get-tuple-element.16.grads_ref, bf16[16,128,128]{2,1,0:T(8,128)(2,1)S(1)} %get-tuple-element.17.fold_ref, s32[32,256]{1,0:T(8,128)S(1)} %bitcast.22, ...), custom_call_target="tpu_custom_call" | custom-call | tf_op jit(solution)/shard_map/tail/pallas_call | solution.py:662
  135.0 2.7 %store.1 = (bf16[32,512,128]{2,1,0:T(8,128)(2,1)}, bf16[8192,128]{1,0:T(8,128)(2,1)}) custom-call(bf16[32,512,128]{2,1,0:T(8,128)(2,1)S(1)} %bitcast.15, bf16[8192,128]{1,0:T(8,128)(2,1)S(1)} %get-tuple-element.19.large_ref), custom_call_target="tpu_custom_call" | custom-call | tf_op jit(solution)/shard_map/store/pallas_call | solution.py:700
  (5 shorter events, 0.0 us)
Async XLA Ops:
  0.6 1.6 %copy-start.2 = (bf16[1,8192,128]{2,1,0:T(8,128)(2,1)S(1)}, bf16[1,8192,128]{2,1,0:T(8,128)(2,1)}, u32[]{:S(2)}) copy-start(bf16[1,8192,128]{2,1,0:T(8,128)(2,1)} %param.15) | copy-start | bytes 6291460
  2.2 0.7 copy-start.5
  2.9 0.8 copy-start.7
  3.7 0.8 copy-start.9
  15.5 2.2 %copy-start = (bf16[32,512,128]{2,1,0:T(8,128)(2,1)S(1)}, bf16[32,512,128]{2,1,0:T(8,128)(2,1)}, u32[]{:S(2)}) copy-start(bf16[32,512,128]{2,1,0:T(8,128)(2,1)} %tables_ref.1) | copy-start | bytes 12582916
  17.7 17.8 %copy-start.4 = (bf16[1304,1024]{1,0:T(8,128)(2,1)S(1)}, bf16[1304,1024]{1,0:T(8,128)(2,1)}, u32[]{:S(2)}) copy-start(bf16[1304,1024]{1,0:T(8,128)(2,1)} %w_ref.1) | copy-start | bytes 8011780
  17.7 17.8 %copy-start.11 = (bf16[256,128]{1,0:T(8,128)(2,1)S(1)}, bf16[256,128]{1,0:T(8,128)(2,1)}, u32[]{:S(2)}) copy-start(bf16[256,128]{1,0:T(8,128)(2,1)} %dense_ref.1) | copy-start | bytes 196612
  17.7 17.8 %copy-start.12 = (s32[16,32]{1,0:T(8,128)S(1)}, s32[16,32]{1,0:T(8,128)}, u32[]{:S(2)}) copy-start(s32[16,32]{1,0:T(8,128)} %sizes_ref.1) | copy-start | bytes 6148
  17.7 17.8 %copy-start.13 = (f32[1024]{0:T(1024)S(1)}, f32[1024]{0:T(1024)}, u32[]{:S(2)}) copy-start(f32[1024]{0:T(1024)} %param.20) | copy-start | bytes 12292
  17.7 17.8 %copy-start.14 = (f32[1024]{0:T(1024)S(1)}, f32[1024]{0:T(1024)}, u32[]{:S(2)}) copy-start(f32[1024]{0:T(1024)} %param.21) | copy-start | bytes 12292
  17.7 17.8 %copy-start.15 = (s32[256]{0:T(256)S(1)}, s32[256]{0:T(256)}, u32[]{:S(2)}) copy-start(s32[256]{0:T(256)} %param.13) | copy-start | bytes 3076
  17.7 41.6 %copy-start.3 = (bf16[1,8192,128]{2,1,0:T(8,128)(2,1)S(1)}, bf16[1,8192,128]{2,1,0:T(8,128)(2,1)}, u32[]{:S(2)}) copy-start(bf16[1,8192,128]{2,1,0:T(8,128)(2,1)} %param.15) | copy-start | bytes 6291460
  35.5 23.8 %copy-start.1 = (bf16[32,512,128]{2,1,0:T(8,128)(2,1)S(1)}, bf16[32,512,128]{2,1,0:T(8,128)(2,1)}, u32[]{:S(2)}) copy-start(bf16[32,512,128]{2,1,0:T(8,128)(2,1)} %tables_ref.1) | copy-start | bytes 12582916
  35.5 23.8 %copy-start.6 = (s32[1,32,128]{2,1,0:T(8,128)S(1)}, s32[1,32,128]{2,1,0:T(8,128)}, u32[]{:S(2)}) copy-start(s32[1,32,128]{2,1,0:T(8,128)} %param.17) | copy-start | bytes 49156
  35.6 23.8 %copy-start.8 = (s32[256,32]{0,1:T(8,128)S(1)}, s32[256,32]{0,1:T(8,128)}, u32[]{:S(2)}) copy-start(s32[256,32]{0,1:T(8,128)} %param.12) | copy-start | bytes 98308
  35.6 23.8 %copy-start.10 = (s32[1,32,256]{2,1,0:T(8,128)S(1)}, s32[1,32,256]{2,1,0:T(8,128)}, u32[]{:S(2)}) copy-start(s32[1,32,256]{2,1,0:T(8,128)} %param.18) | copy-start | bytes 98308

commit v3 on v2

--- a/solution.py
+++ b/solution.py
@@ -20,9 +20,16 @@
     return pl.BlockSpec(memory_space=space)
 
 
+def size_of(*arrays):
+    return sum(math.prod(a.shape) * jnp.dtype(a.dtype).itemsize for a in arrays)
+
+
 def grant(*arrays):
-    total = sum(math.prod(a.shape) * jnp.dtype(a.dtype).itemsize for a in arrays)
-    return min(VMEM_LIMIT, total + 6 * MIB)
+    return min(VMEM_LIMIT, size_of(*arrays) + 6 * MIB)
+
+
+def all_but(*arrays):
+    return min(VMEM_LIMIT, 63 * MIB - size_of(*arrays))
 
 
 def iota(shape, axis):
@@ -34,60 +41,6 @@
     starts = jnp.where(iota((1, span), 1) == 0, 0, pltpu.roll(ends, 1, 1))
     places = iota((slots, span), 0)
     return ((places >= starts) & (places < ends)).astype(f32).astype(bf16)
-
-
-def pool_kernel(
-    first_ref, rows_ref, count_ref, ends_ref, table_ref, ids_ref, out_ref, by_sample, wide, picked,
-):
-    by_sample[...] = jnp.transpose(ids_ref[...])
-    slots = rows_ref.shape[1]
-    owners = out_ref.shape[0]
-    last = count_ref.shape[1] - 1
-    first = first_ref[0]
-    wide[...] = table_ref[...].astype(f32)
-    picked[...] = jnp.zeros_like(picked)
-
-    def owner(o, carry):
-        d = o + first
-
-        def group(g, c):
-            base = pl.multiple_of(g * 8, 8)
-            parts = [wide[pl.ds(rows_ref[d, base + u], 1), :] for u in range(8)]
-            picked[pl.ds(pl.multiple_of(o * slots + base, 8), 8), :] = jnp.concatenate(parts, axis=0)
-            return c
-
-        return lax.fori_loop(0, (count_ref[d, last] + 7) // 8, group, carry)
-
-    lax.fori_loop(0, owners, owner, 0)
-
-    def sums(o, carry):
-        members = members_of(ends_ref[pl.ds(o + first, 1), :], slots)
-        block = picked[pl.ds(pl.multiple_of(o * slots, 8), slots), :].astype(bf16)
-        pooled = lax.dot_general(
-            members, block, (((0,), (0,)), ((), ())), preferred_element_type=f32
-        )
-        out_ref[o] = pooled.astype(bf16)
-        return carry
-
-    lax.fori_loop(0, owners, sums, 0, unroll=4)
-
-
-def pool(first, owners, rows, ends, table, ids):
-    slots = rows.shape[1]
-    width = table.shape[1]
-    scratch = [pltpu.VMEM(table.shape, f32), pltpu.VMEM((owners * slots, width), f32)]
-    return pl.pallas_call(
-        pool_kernel,
-        out_shape=(
-            jax.ShapeDtypeStruct((owners, ends.shape[1], width), bf16),
-            jax.ShapeDtypeStruct((ids.shape[1], ids.shape[0]), ids.dtype),
-        ),
-        in_specs=[whole(pltpu.SMEM)] * 3 + [whole(pltpu.VMEM)] * 3,
-        out_specs=(whole(pltpu.VMEM),) * 2,
-        scratch_shapes=scratch,
-        compiler_params=pltpu.CompilerParams(vmem_limit_bytes=grant(table, ids, ids, ends, *scratch)),
-        name="pool",
-    )(first, rows, ends, ends, table, ids)
 
 
 def spans_of(vec_count):
@@ -277,65 +230,98 @@
     )
 
 
-def forward_kernel(pooled_ref, own_ids_ref, tables_ref, large_out, small_out, send, recv, own, tables):
+def head_kernel(
+    rows_hbm, ends_hbm, ids_hbm, table_hbm, tables_hbm, large_out, small_out,
+    rows, ends, ids, narrow, wide, tables, by_sample, outbox, send, recv, local,
+):
     groups = lax.axis_size("shard")
     rep, me = lax.axis_index("rep"), lax.axis_index("shard")
-
-    def block(k):
-        to = lax.rem(me + k, groups)
-        return remote(pooled_ref.at[to], large_out.at[me], send.at[k], recv.at[k], rep, to)
-
-    def block_in(k):
-        at = lax.rem(me + groups - k, groups)
-        return remote(pooled_ref.at[at], large_out.at[at], send.at[k], recv.at[k], rep, at)
-
-    def run(low, high, act):
+    slots = rows.shape[1]
+    arrays = ((rows_hbm, rows), (ends_hbm, ends), (ids_hbm, ids), (table_hbm, narrow), (tables_hbm, tables))
+    fetch = [pltpu.make_async_copy(src, dst, local.at[n]) for n, (src, dst) in enumerate(arrays)]
+    for copy in fetch:
+        copy.start()
+    greet_all()
+    for copy in fetch[:4]:
+        copy.wait()
+    wide[...] = narrow[...].astype(f32)
+
+    def block(off):
+        to = lax.rem(me + off, groups)
+        return remote(outbox.at[to], large_out.at[me], send.at[off], recv.at[off], rep, to)
+
+    def block_in(off):
+        at = lax.rem(me + groups - off, groups)
+        return remote(outbox.at[at], large_out.at[at], send.at[off], recv.at[off], rep, at)
+
+    def loop(low, high, act):
         def body(k, c):
             act(k)
             return c
 
         lax.fori_loop(low, high, body, 0)
 
-    fetch = pltpu.make_async_copy(tables_ref, tables, own.at[1])
-    fetch.start()
-    greet_all()
-    run(1, groups, lambda k: block(k).start())
-    mine = pltpu.make_async_copy(pooled_ref.at[me], large_out.at[me], own.at[0])
-    mine.start()
-    batch, small_count = own_ids_ref.shape
-    rows = iota((batch, tables_ref.shape[1]), 1)
-    fetch.wait()
-    for t in range(small_count):
-        hot = (own_ids_ref[:, t : t + 1] == rows).astype(f32).astype(bf16)
+    def give(i):
+        off = lax.rem(groups // 2 + i, groups)
+        to = lax.rem(me + off, groups)
+        d = rep * groups + to
+        picked = [
+            jnp.concatenate([wide[pl.ds(rows[d, s + u], 1), :] for u in range(8)], axis=0)
+            for s in range(0, slots, 8)
+        ]
+        pooled = lax.dot_general(
+            members_of(ends[pl.ds(d, 1), :], slots), jnp.concatenate(picked, axis=0).astype(bf16),
+            (((0,), (0,)), ((), ())), preferred_element_type=f32,
+        )
+        outbox[to] = pooled.astype(bf16)
+
+        @pl.when(off != 0)
+        def _():
+            block(off).start()
+
+    loop(0, groups, give)
+    by_sample[...] = jnp.transpose(ids[...])
+    large_out[me] = outbox[me]
+    fetch[4].wait()
+    at_row = iota((by_sample.shape[0], tables.shape[1]), 1)
+    for t in range(tables.shape[0]):
+        hot = (by_sample[:, t : t + 1] == at_row).astype(f32).astype(bf16)
         small_out[t] = jnp.dot(hot, tables[t], preferred_element_type=f32).astype(bf16)
-    mine.wait()
-    run(1, groups, lambda k: block_in(k).wait_recv())
-    run(1, groups, lambda k: block(k).wait_send())
-
-
-def forward(pooled, own_ids, tables):
-    groups = pooled.shape[0]
-    small = jax.ShapeDtypeStruct(
-        (tables.shape[0], own_ids.shape[0], tables.shape[2]), tables.dtype
-    )
+    loop(1, groups, lambda off: block_in(off).wait_recv())
+    loop(1, groups, lambda off: block(off).wait_send())
+
+
+def head(groups, rows, ends, ids, table, tables, w_first):
+    large = jax.ShapeDtypeStruct((groups, ends.shape[1], table.shape[1]), bf16)
+    small = jax.ShapeDtypeStruct((tables.shape[0], ids.shape[1], tables.shape[2]), tables.dtype)
+    scratch = [
+        pltpu.VMEM(ends.shape, ends.dtype),
+        pltpu.VMEM(ids.shape, ids.dtype),
+        pltpu.VMEM(table.shape, table.dtype),
+        pltpu.VMEM(table.shape, f32),
+        pltpu.VMEM(tables.shape, tables.dtype),
+        pltpu.VMEM((ids.shape[1], ids.shape[0]), ids.dtype),
+        pltpu.VMEM(large.shape, bf16),
+    ]
+    dma = pltpu.SemaphoreType.DMA
     return pl.pallas_call(
-        forward_kernel,
-        out_shape=(jax.ShapeDtypeStruct(pooled.shape, pooled.dtype), small),
-        in_specs=[whole(pltpu.VMEM)] * 2 + [whole(pl.ANY)],
+        head_kernel,
+        out_shape=(large, small),
+        in_specs=[whole(pltpu.HBM)] * 5,
         out_specs=(whole(pltpu.VMEM),) * 2,
-        scratch_shapes=[pltpu.SemaphoreType.DMA((groups,))] * 2
-        + [pltpu.SemaphoreType.DMA((2,)), pltpu.VMEM(tables.shape, tables.dtype)],
+        scratch_shapes=[pltpu.SMEM(rows.shape, rows.dtype)] + scratch
+        + [dma((groups,)), dma((groups,)), dma((5,))],
         compiler_params=pltpu.CompilerParams(
             collective_id=0, has_side_effects=True,
-            vmem_limit_bytes=grant(pooled, pooled, own_ids, tables, small),
+            vmem_limit_bytes=max(grant(large, small, *scratch), all_but(large, small, w_first)),
         ),
-        name="forward",
-    )(pooled, own_ids, tables)
+        name="head",
+    )(rows, ends, ids, table, tables)
 
 
 def tail_kernel(
     ids_ref, grads_ref, fold_ref, rows_ref, ends_ref, table_ref, tables_ref, small_out, large_out,
-    peer_ids, peer_grads, folds, acc, lhs, rhs, keep, sent, came, sent_2, came_2, sent_3, came_3,
+    peer_ids, peer_grads, folds, acc, lhs_0, lhs_1, rhs_0, rhs_1, keep, sent, came, sent_2, came_2, sent_3, came_3,
     prior, local, peer_s, peer_r, fold_s, fold_r, far_s, far_r, rs1_s, rs1_r, rs2_s, rs2_r,
     rs3_s, rs3_r, ag_z, ag_1, ag_2, ag_core, ag_r,
 ):
@@ -462,7 +448,7 @@
 
     spot = iota((spots, slots), 0)
 
-    def spread_one(d, v):
+    def place_rows(d, v, lhs, rhs):
         members = members_of(ends_ref[pl.ds(d, 1), :], slots)
         moved = jnp.dot(members, folds[d], preferred_element_type=f32)
         at = rows_ref[pl.ds(d, 1), :]
@@ -474,44 +460,52 @@
             ).astype(bf16)
         lhs[:, v * slots : (v + 1) * slots] = (spot == at - block * spots).astype(f32).astype(bf16)
 
-    step = 2 * width
-
-    def spread_pair(d, e):
-        spread_one(d, 0)
-        spread_one(e, 1)
-
-        def add(n):
-            at = pl.ds(pl.multiple_of(n * step, step), step)
-            acc[:, at] += jnp.dot(lhs[...], rhs[:, at], preferred_element_type=f32)
-
-        loop(0, acc.shape[1] // step, add)
-
     def take(k):
         in_block(k).wait_recv()
         far_out(k).start()
 
-    def near(k):
-        return rep * groups + lax.rem(me + groups - k, groups)
-
-    def near_pair(p):
-        @pl.when(p > 0)
+    def get(p):
+        @pl.when((p > 0) & (p < groups // 2))
         def _():
             take(2 * p)
 
-        take(2 * p + 1)
-        spread_pair(near(2 * p), near(2 * p + 1))
-
-    def far_pair(p):
-        far_in(2 * p).wait_recv()
-        far_in(2 * p + 1).wait_recv()
-        spread_pair(
-            other * groups + lax.rem(me + groups - 2 * p, groups),
-            other * groups + lax.rem(me + groups - 2 * p - 1, groups),
-        )
-
-    pairs = groups // 2
-    cut_1, cut_2 = pairs * 3 // 8, pairs // 2
-    loop(0, cut_1, near_pair)
+        @pl.when(p < groups // 2)
+        def _():
+            take(2 * p + 1)
+
+        @pl.when((p >= groups // 2) & (p < groups))
+        def _():
+            far_in(2 * p - groups).wait_recv()
+            far_in(2 * p + 1 - groups).wait_recv()
+
+    def owner(k):
+        side = k // groups
+        at = lax.rem(me + groups - (k - side * groups), groups)
+        return (rep + side * (1 - 2 * rep)) * groups + at
+
+    step = 2 * width
+
+    def make(p, lhs, rhs):
+        place_rows(owner(2 * p), 0, lhs, rhs)
+        place_rows(owner(2 * p + 1), 1, lhs, rhs)
+
+    def multiply(lhs, rhs):
+        for n in range(0, acc.shape[1], step):
+            acc[:, n : n + step] += jnp.dot(lhs[...], rhs[:, n : n + step], preferred_element_type=f32)
+
+    def pairs(i):
+        get(2 * i + 1)
+        make(2 * i + 1, lhs_1, rhs_1)
+        multiply(lhs_0, rhs_0)
+        get(2 * i + 2)
+        make(jnp.minimum(2 * i + 2, groups - 1), lhs_0, rhs_0)
+        multiply(lhs_1, rhs_1)
+
+    turns = groups // 2
+    cut_1, cut_2, cut_3 = turns // 8, turns // 2, turns * 7 // 8
+    get(0)
+    make(0, lhs_0, rhs_0)
+    loop(0, cut_1, pairs)
 
     def turn(h):
         first_hop(h, 0).wait_recv()
@@ -519,7 +513,7 @@
         second_hop(h).start()
 
     loop(0, 2, turn)
-    loop(cut_1, pairs, near_pair)
+    loop(cut_1, cut_2, pairs)
 
     def along(h):
         first_hop(h, 1).wait_recv()
@@ -530,7 +524,7 @@
         loop(1, ring, lambda k: third_hop(h, k).start())
 
     loop(0, 2, along)
-    loop(0, cut_2, far_pair)
+    loop(cut_2, cut_3, pairs)
 
     for copy in fetch:
         copy.wait()
@@ -586,7 +580,7 @@
         third(h, 0, rep, z, y)
         last(h, 0, rep, z, y)
 
-    loop(cut_2, pairs, far_pair)
+    loop(cut_3, turns, pairs)
     for q in range(blocks):
         at = slice(q * spots, (q + 1) * spots)
         large_out[at, :] = (
@@ -648,6 +642,8 @@
         pltpu.VMEM((devices,) + fold.shape[1:], bf16),
         pltpu.VMEM((table.shape[0] // blocks, blocks * width), f32),
         pltpu.VMEM((table.shape[0] // blocks, 2 * slots), bf16),
+        pltpu.VMEM((table.shape[0] // blocks, 2 * slots), bf16),
+        pltpu.VMEM((2 * slots, blocks * width), bf16),
         pltpu.VMEM((2 * slots, blocks * width), bf16),
         pltpu.VMEM((2, 2, unit, width), f32),
         pltpu.VMEM((2, 2, unit, width), bf16),
@@ -716,13 +712,11 @@
     owner_row_index, w_first, b_first, w_out,
 ):
     groups = lax.axis_size("shard")
-    first = lax.axis_index("rep") * groups
-    index = first + lax.axis_index("shard")
+    index = lax.axis_index("rep") * groups + lax.axis_index("shard")
     ends, rows, table = bag_ends[0], owner_row_index[0], large_tables[0]
     ids = jnp.transpose(small_ids)
 
-    pooled, own_ids = pool(first[None], groups, rows, ends, table, ids)
-    large, small = forward(pooled, own_ids, small_tables)
+    large, small = head(groups, rows, ends, ids, table, small_tables, w_first)
     small_grads, fold = top(
         index[None], batch_sizes, dense, labels, small, large, w_first, b_first, w_out
     )

time: 139 us -> 120 us (0.86)
  Pallas kernels: 131 us -> 114 us
  local copies, waits for them, and re-layouts: 6.06 us -> 2.67 us
    pallas_call x1, Pallas kernels: 75.6 us -> 65.5 us  [tail(): pl.pallas_call(tail_kernel, out_shape=(jax.ShapeDtypeStruct(split, bf16),...]
    pallas_call x2 -> x1, Pallas kernels: 28.8 us -> 22 us  [head(): pl.pallas_call(head_kernel, out_shape=(large, small), in_specs=[whole(plt...]
    unnamed x32 -> x26, local copies, waits for them, and re-layouts: 6.06 us -> 2.67 us
where the time goes in v3:
time: 120 us; the launch traced here: 118 us
  Pallas kernels  114 us (95%)
  local copies, waits for them, and re-layouts  2.67 us (2%)
    pallas_call x1, Pallas kernels, tail(): pl.pallas_call(tail_kernel, out_shape=(jax.ShapeDtypeStruct(split, bf16),...  65.5 us
    pallas_call x1, Pallas kernels, top(): pl.pallas_call(functools.partial(top_kernel, vec_count, pad), out_shape=(...  23.7 us
    pallas_call x1, Pallas kernels, head(): pl.pallas_call(head_kernel, out_shape=(large, small), in_specs=[whole(plt...  22 us
    pallas_call x1, Pallas kernels, store(): pl.pallas_call(store_kernel, out_shape=(jax.ShapeDtypeStruct(small.shape,...  2.72 us
    unnamed x26, local copies, waits for them, and re-layouts  2.67 us

profile of v3, /device:TPU:1, one launch (start us, length us, event | category | flops | bytes accessed | tf_op | source)
XLA Modules:
  0.0 117.6 jit_solution(9307575818415126264)
XLA Ops:
  0.6 0.0 copy-start.2
  0.6 0.0 copy-start.7
  0.7 0.0 copy-start.9
  0.7 0.0 copy-start.10
  0.7 0.0 copy-start.11
  0.7 0.0 copy-start.12
  0.7 0.0 copy-start.1
  0.7 22.0 %head.1 = (bf16[16,128,128]{2,1,0:T(8,128)(2,1)}, bf16[32,256,128]{2,1,0:T(8,128)(2,1)}) custom-call(s32[32,256]{1,0:T(8,128)} %bitcast.17, s32[32,128]{1,0:T(8,128)} %bitcast.19, s32[32,256]{1,0:T(8,128)} %bitcast.15, bf16[8192,128]{1,0:T(8,128)(2,1)} %bitcast.12, bf16[32,512,128]{2,1,0:T(8,128)(2,1)} %tables_hbm.1), custom_call_target="tpu_custom_call" | custom-call | tf_op jit(solution)/shard_map/head/pallas_call | solution.py:307
  22.7 0.0 copy-done.2
  22.7 0.0 copy-done.7
  22.7 0.0 copy-done.9
  22.8 0.0 copy-done.10
  22.8 0.0 copy-done.11
  22.8 0.0 copy-done.12
  22.8 0.0 copy-start.3
  22.8 1.6 %copy-done.3 = bf16[32,256,128]{2,1,0:T(8,128)(2,1)S(1)} copy-done((bf16[32,256,128]{2,1,0:T(8,128)(2,1)S(1)}, bf16[32,256,128]{2,1,0:T(8,128)(2,1)}, u32[]{:S(2)}) %copy-start.3) | copy-done | bytes 2097176
  24.4 0.0 copy-start.4
  24.4 1.0 copy-done.4
  25.4 0.0 copy-start
  25.4 0.0 copy-start.5
  25.4 0.0 copy-start.6
  25.4 0.0 copy-start.8
  25.4 23.7 %top.1 = (bf16[32,256,128]{2,1,0:T(8,128)(2,1)S(1)}, bf16[16,128,128]{2,1,0:T(8,128)(2,1)S(1)}) custom-call(s32[1]{0:T(128)} %bitcast.1.index_ref, s32[16,32]{1,0:T(8,128)S(1)} %copy-done.9, bf16[256,128]{1,0:T(8,128)(2,1)S(1)} %copy-done.7, s32[1,256]{1,0:T(1,128)S(1)} %bitcast.23, bf16[32,256,128]{2,1,0:T(8,128)(2,1)S(1)} %copy-done.3, ...), custom_call_target="tpu_custom_call" | custom-call | tf_op jit(solution)/shard_map/top/pallas_call | solution.py:189
  49.2 0.0 copy-done.1
  49.2 0.0 copy-done
  49.2 0.0 copy-done.5
  49.2 0.0 copy-done.6
  49.2 0.0 copy-done.8
  49.2 65.5 %tail.1 = (bf16[2,2,2,2,4,256,128]{6,5,4,3,2,1,0:T(8,128)(2,1)S(1)}, bf16[8192,128]{1,0:T(8,128)(2,1)S(1)}) custom-call(s32[32,256]{1,0:T(8,128)S(1)} %bitcast.16, bf16[32,256,128]{2,1,0:T(8,128)(2,1)S(1)} %get-tuple-element.12.grads_ref, bf16[16,128,128]{2,1,0:T(8,128)(2,1)S(1)} %get-tuple-element.13.fold_ref, s32[32,256]{1,0:T(8,128)S(1)} %bitcast.18, ...), custom_call_target="tpu_custom_call" | custom-call | tf_op jit(solution)/shard_map/tail/pallas_call | solution.py:658
  114.7 2.7 %store.1 = (bf16[32,512,128]{2,1,0:T(8,128)(2,1)}, bf16[8192,128]{1,0:T(8,128)(2,1)}) custom-call(bf16[32,512,128]{2,1,0:T(8,128)(2,1)S(1)} %bitcast.14, bf16[8192,128]{1,0:T(8,128)(2,1)S(1)} %get-tuple-element.15.large_ref), custom_call_target="tpu_custom_call" | custom-call | tf_op jit(solution)/shard_map/store/pallas_call | solution.py:696
Async XLA Ops:
  0.6 22.1 %copy-start.2 = (bf16[1304,1024]{1,0:T(8,128)(2,1)S(1)}, bf16[1304,1024]{1,0:T(8,128)(2,1)}, u32[]{:S(2)}) copy-start(bf16[1304,1024]{1,0:T(8,128)(2,1)} %w_ref.1) | copy-start | bytes 8011780
  0.6 22.1 %copy-start.7 = (bf16[256,128]{1,0:T(8,128)(2,1)S(1)}, bf16[256,128]{1,0:T(8,128)(2,1)}, u32[]{:S(2)}) copy-start(bf16[256,128]{1,0:T(8,128)(2,1)} %dense_ref.1) | copy-start | bytes 196612
  0.7 22.1 %copy-start.9 = (s32[16,32]{1,0:T(8,128)S(1)}, s32[16,32]{1,0:T(8,128)}, u32[]{:S(2)}) copy-start(s32[16,32]{1,0:T(8,128)} %sizes_ref.1) | copy-start | bytes 6148
  0.7 22.1 %copy-start.10 = (f32[1024]{0:T(1024)S(1)}, f32[1024]{0:T(1024)}, u32[]{:S(2)}) copy-start(f32[1024]{0:T(1024)} %param.20) | copy-start | bytes 12292
  0.7 22.1 %copy-start.11 = (f32[1024]{0:T(1024)S(1)}, f32[1024]{0:T(1024)}, u32[]{:S(2)}) copy-start(f32[1024]{0:T(1024)} %param.21) | copy-start | bytes 12292
  0.7 22.1 %copy-start.12 = (s32[256]{0:T(256)S(1)}, s32[256]{0:T(256)}, u32[]{:S(2)}) copy-start(s32[256]{0:T(256)} %param.13) | copy-start | bytes 3076
  0.7 48.5 %copy-start.1 = (bf16[1,8192,128]{2,1,0:T(8,128)(2,1)S(1)}, bf16[1,8192,128]{2,1,0:T(8,128)(2,1)}, u32[]{:S(2)}) copy-start(bf16[1,8192,128]{2,1,0:T(8,128)(2,1)} %param.15) | copy-start | bytes 6291460
  22.8 1.6 %copy-start.3 = (bf16[32,256,128]{2,1,0:T(8,128)(2,1)S(1)}, bf16[32,256,128]{2,1,0:T(8,128)(2,1)}, u32[]{:S(2)}) copy-start(bf16[32,256,128]{2,1,0:T(8,128)(2,1)} %get-tuple-element.10.small_ref) | copy-start | bytes 6291460
  24.4 1.0 copy-start.4
  25.4 23.7 %copy-start = (bf16[32,512,128]{2,1,0:T(8,128)(2,1)S(1)}, bf16[32,512,128]{2,1,0:T(8,128)(2,1)}, u32[]{:S(2)}) copy-start(bf16[32,512,128]{2,1,0:T(8,128)(2,1)} %tables_hbm.1) | copy-start | bytes 12582916
  25.4 23.8 %copy-start.5 = (s32[256,32]{0,1:T(8,128)S(1)}, s32[256,32]{0,1:T(8,128)}, u32[]{:S(2)}) copy-start(s32[256,32]{0,1:T(8,128)} %param.12) | copy-start | bytes 98308
  25.4 23.8 %copy-start.6 = (s32[1,32,256]{2,1,0:T(8,128)S(1)}, s32[1,32,256]{2,1,0:T(8,128)}, u32[]{:S(2)}) copy-start(s32[1,32,256]{2,1,0:T(8,128)} %param.18) | copy-start | bytes 98308
  25.4 23.8 %copy-start.8 = (s32[1,32,128]{2,1,0:T(8,128)S(1)}, s32[1,32,128]{2,1,0:T(8,128)}, u32[]{:S(2)}) copy-start(s32[1,32,128]{2,1,0:T(8,128)} %param.17) | copy-start | bytes 49156

commit v4 on v3

--- a/solution.py
+++ b/solution.py
@@ -48,7 +48,7 @@
 
 
 def top_kernel(
-    vec_count, pad, index_ref, sizes_ref, dense_ref, labels_ref, small_ref, large_ref,
+    vec_count, group, pad, index_ref, sizes_ref, dense_ref, labels_ref, small_ref, large_ref,
     w_ref, bias_ref, wout_ref, small_out, fold_out, vecs, gram, pairs, spread,
 ):
     batch, width = dense_ref.shape
@@ -78,53 +78,64 @@
 
     unroll = 8
 
+    many = batch // group
+    tall = group * pad
+
     def gram_step(g, c):
         for u in range(unroll):
-            at = pl.ds(pl.multiple_of((g * unroll + u) * pad, 8), pad)
+            at = pl.ds(pl.multiple_of((g * unroll + u) * tall, 8), tall)
             own = vecs[at, :].astype(bf16)
-            gram[at, 0:pad] = lax.dot_general(
+            gram[at, 0:tall] = lax.dot_general(
                 own, own, (((1,), (1,)), ((), ())), preferred_element_type=f32
             )
         return c
 
-    lax.fori_loop(0, batch // unroll, gram_step, 0)
+    lax.fori_loop(0, many // unroll, gram_step, 0)
 
     lane = iota((1, LANES), 1)
     chunk = 64
-    for start in range(0, batch, chunk):
+    places = [(v, start) for v in range(group) for start in range(0, many, chunk)]
+
+    def strided(v, start, i, size):
+        return pl.ds((start * group + v) * pad + i, size, stride=tall)
+
+    for v, start in places:
         tile = jnp.zeros((chunk, LANES), f32)
         at_tile = 0
+        row = v * many + start
         for i, off in spans:
-            piece = gram[pl.ds(start * pad + i, chunk, stride=pad), :]
-            turn = off % LANES
+            piece = gram[strided(v, start, i, chunk), :]
+            turn = (off - v * pad) % LANES
             if turn:
                 piece = pltpu.roll(piece, turn, 1)
             low = off - at_tile * LANES
             tile = jnp.where((lane >= low) & (lane < low + i), piece, tile)
             if low + i >= LANES:
-                pairs[start : start + chunk, at_tile * LANES : (at_tile + 1) * LANES] = (
+                pairs[row : row + chunk, at_tile * LANES : (at_tile + 1) * LANES] = (
                     tile * scale
                 ).astype(bf16)
                 at_tile += 1
                 rest = low + i - LANES
                 tile = jnp.where(lane < rest, piece, jnp.zeros_like(piece))
         if at_tile * LANES < pair_pad:
-            pairs[start : start + chunk, at_tile * LANES : pair_pad] = (tile * scale).astype(bf16)
-
-    block = 128
-    labels_col = jnp.transpose(
+            pairs[row : row + chunk, at_tile * LANES : pair_pad] = (tile * scale).astype(bf16)
+
+    block = min(128, many)
+    gram[0:batch, :] = jnp.transpose(
         jnp.broadcast_to(labels_ref[...].astype(f32), (LANES, batch))
-    )[:, 0:1]
-    for start in range(0, batch, block):
-        at = slice(start, start + block)
+    )
+    labels_of = [gram[pl.ds(v, many, stride=group), :][:, 0:1] for v in range(group)]
+    for v, start in [(v, start) for v in range(group) for start in range(0, many, block)]:
+        at = slice(v * many + start, v * many + start + block)
+        own_dense = vecs[strided(v, start, 0, block), :].astype(bf16)
         preact = (
             jnp.dot(pairs[at, :], w_ref[0:pair_pad, :], preferred_element_type=f32)
-            + jnp.dot(dense_ref[at, :], w_ref[pair_count : pair_count + width, :], preferred_element_type=f32)
+            + jnp.dot(own_dense, w_ref[pair_count : pair_count + width, :], preferred_element_type=f32)
             + bias_ref[...]
         )
         squash = jax.nn.sigmoid(preact)
         logits = jnp.sum(preact * squash * wout_ref[...], axis=1, keepdims=True)
-        grad = jax.nn.sigmoid(logits) - labels_col[at, :]
+        grad = jax.nn.sigmoid(logits) - labels_of[v][start : start + block, :]
         pre_grad = (
             grad * wout_ref[...] * (squash * (1.0 + preact * (1.0 - squash)))
         ).astype(bf16)
@@ -137,29 +148,33 @@
     gram[rows_of(0), :] = jnp.zeros((batch, LANES), f32)
     for i in range(vec_count, pad):
         gram[rows_of(i), :] = jnp.zeros((batch, LANES), f32)
-    for start in range(0, batch, chunk):
+    for v, start in places:
+        row = v * many + start
         for i, off in spans:
             first = off // LANES
             low = off - first * LANES
-            here = spread[start : start + chunk, first * LANES : (first + 1) * LANES]
+            here = spread[row : row + chunk, first * LANES : (first + 1) * LANES]
             if low + i > LANES:
-                after = spread[start : start + chunk, (first + 1) * LANES : (first + 2) * LANES]
+                after = spread[row : row + chunk, (first + 1) * LANES : (first + 2) * LANES]
                 here = jnp.where(lane >= low, here, after)
-            if low:
-                here = pltpu.roll(here, LANES - low, 1)
-            gram[pl.ds(start * pad + i, chunk, stride=pad), :] = jnp.where(lane < i, here, 0.0)
+            turn = (v * pad - low) % LANES
+            if turn:
+                here = pltpu.roll(here, turn, 1)
+            gram[strided(v, start, i, chunk), :] = jnp.where(
+                (lane >= v * pad) & (lane < v * pad + i), here, 0.0
+            )
 
     def back_step(g, c):
         for u in range(unroll):
-            at = pl.ds(pl.multiple_of((g * unroll + u) * pad, 8), pad)
+            at = pl.ds(pl.multiple_of((g * unroll + u) * tall, 8), tall)
             lower = gram[at, :]
-            both = lower[:, 0:pad] + jnp.transpose(lower)[0:pad, :]
+            both = lower[:, 0:tall] + jnp.transpose(lower)[0:tall, :]
             vecs[at, :] = jnp.dot(
                 both.astype(bf16), vecs[at, :].astype(bf16), preferred_element_type=f32
             )
         return c
 
-    lax.fori_loop(0, batch // unroll, back_step, 0)
+    lax.fori_loop(0, many // unroll, back_step, 0)
 
     for t in range(small_count):
         small_out[t] = vecs[rows_of(1 + t), :].astype(bf16)
@@ -177,7 +192,11 @@
     batch, width = dense.shape
     small_count, feats, bag_span = small.shape[0], large.shape[0], large.shape[1]
     vec_count = 1 + small_count + feats
-    pad = -(-vec_count // 8) * 8
+    group = max(1, LANES // (-(-vec_count // 8) * 8))
+    tiles = -(-group * vec_count // 8)
+    if tiles % 2 == 0 and (tiles + 1) * 8 <= LANES:
+        tiles += 1
+    pad = tiles * 8 // group
     pair_count = vec_count * (vec_count - 1) // 2
     pair_pad = -(-pair_count // LANES) * LANES
     scratch = [
@@ -187,7 +206,7 @@
         pltpu.VMEM((batch, pair_pad), f32),
     ]
     return pl.pallas_call(
-        functools.partial(top_kernel, vec_count, pad),
+        functools.partial(top_kernel, vec_count, group, pad),
         out_shape=(
             jax.ShapeDtypeStruct((small_count, batch, width), bf16),
             jax.ShapeDtypeStruct((feats, bag_span, width), bf16),
@@ -460,9 +479,15 @@
             ).astype(bf16)
         lhs[:, v * slots : (v + 1) * slots] = (spot == at - block * spots).astype(f32).astype(bf16)
 
+    turns = groups // 2
+    cut_1, cut_2, cut_3 = turns // 4, turns // 2, turns * 7 // 8
+
     def take(k):
         in_block(k).wait_recv()
-        far_out(k).start()
+
+        @pl.when(k > 4 * cut_1 + 1)
+        def _():
+            far_out(k).start()
 
     def get(p):
         @pl.when((p > 0) & (p < groups // 2))
@@ -501,9 +526,7 @@
         make(jnp.minimum(2 * i + 2, groups - 1), lhs_0, rhs_0)
         multiply(lhs_1, rhs_1)
 
-    turns = groups // 2
-    cut_1, cut_2, cut_3 = turns // 8, turns // 2, turns * 7 // 8
-    get(0)
+    loop(0, 1, get)
     make(0, lhs_0, rhs_0)
     loop(0, cut_1, pairs)
 
@@ -513,6 +536,7 @@
         second_hop(h).start()
 
     loop(0, 2, turn)
+    loop(1, 4 * cut_1 + 2, lambda k: far_out(k).start())
     loop(cut_1, cut_2, pairs)
 
     def along(h):

time: 120 us -> 113 us (0.942)
  Pallas kernels: 114 us -> 107 us
    pallas_call x1, Pallas kernels: 23.7 us -> 17.5 us  [top(): pl.pallas_call(functools.partial(top_kernel, vec_count, group, pad), out_...]
where the time goes in v4:
time: 113 us; the launch traced here: 111 us
  Pallas kernels  107 us (95%)
  local copies, waits for them, and re-layouts  2.67 us (2%)
    pallas_call x1, Pallas kernels, tail(): pl.pallas_call(tail_kernel, out_shape=(jax.ShapeDtypeStruct(split, bf16),...  65.2 us
    pallas_call x1, Pallas kernels, head(): pl.pallas_call(head_kernel, out_shape=(large, small), in_specs=[whole(plt...  22 us
    pallas_call x1, Pallas kernels, top(): pl.pallas_call(functools.partial(top_kernel, vec_count, group, pad), out_...  17.5 us
    pallas_call x1, Pallas kernels, store(): pl.pallas_call(store_kernel, out_shape=(jax.ShapeDtypeStruct(small.shape,...  2.72 us
    unnamed x26, local copies, waits for them, and re-layouts  2.67 us

profile of v4, /device:TPU:1, one launch (start us, length us, event | category | flops | bytes accessed | tf_op | source)
XLA Modules:
  0.0 111.1 jit_solution(17214029419480293761)
XLA Ops:
  0.6 0.0 copy-start.2
  0.6 0.0 copy-start.7
  0.7 0.0 copy-start.9
  0.7 0.0 copy-start.10
  0.7 0.0 copy-start.11
  0.7 0.0 copy-start.12
  0.7 0.0 copy-start.1
  0.7 22.0 %head.1 = (bf16[16,128,128]{2,1,0:T(8,128)(2,1)}, bf16[32,256,128]{2,1,0:T(8,128)(2,1)}) custom-call(s32[32,256]{1,0:T(8,128)} %bitcast.17, s32[32,128]{1,0:T(8,128)} %bitcast.19, s32[32,256]{1,0:T(8,128)} %bitcast.15, bf16[8192,128]{1,0:T(8,128)(2,1)} %bitcast.12, bf16[32,512,128]{2,1,0:T(8,128)(2,1)} %tables_hbm.1), custom_call_target="tpu_custom_call" | custom-call | tf_op jit(solution)/shard_map/head/pallas_call | solution.py:326
  22.7 0.0 copy-done.2
  22.7 0.0 copy-done.7
  22.7 0.0 copy-done.9
  22.8 0.0 copy-done.10
  22.8 0.0 copy-done.11
  22.8 0.0 copy-done.12
  22.8 0.0 copy-start.3
  22.8 1.6 %copy-done.3 = bf16[32,256,128]{2,1,0:T(8,128)(2,1)S(1)} copy-done((bf16[32,256,128]{2,1,0:T(8,128)(2,1)S(1)}, bf16[32,256,128]{2,1,0:T(8,128)(2,1)}, u32[]{:S(2)}) %copy-start.3) | copy-done | bytes 2097176
  24.4 0.0 copy-start.4
  24.4 1.0 copy-done.4
  25.4 0.0 copy-start
  25.4 0.0 copy-start.5
  25.4 0.0 copy-start.6
  25.4 0.0 copy-start.8
  25.4 17.5 %top.1 = (bf16[32,256,128]{2,1,0:T(8,128)(2,1)S(1)}, bf16[16,128,128]{2,1,0:T(8,128)(2,1)S(1)}) custom-call(s32[1]{0:T(128)} %bitcast.1.index_ref, s32[16,32]{1,0:T(8,128)S(1)} %copy-done.9, bf16[256,128]{1,0:T(8,128)(2,1)S(1)} %copy-done.7, s32[1,256]{1,0:T(1,128)S(1)} %bitcast.23, bf16[32,256,128]{2,1,0:T(8,128)(2,1)S(1)} %copy-done.3, ...), custom_call_target="tpu_custom_call" | custom-call | tf_op jit(solution)/shard_map/top/pallas_call | solution.py:208
  42.9 0.0 copy-done.1
  42.9 0.0 copy-done
  42.9 0.0 copy-done.5
  42.9 0.0 copy-done.6
  42.9 0.0 copy-done.8
  43.0 65.2 %tail.1 = (bf16[2,2,2,2,4,256,128]{6,5,4,3,2,1,0:T(8,128)(2,1)S(1)}, bf16[8192,128]{1,0:T(8,128)(2,1)S(1)}) custom-call(s32[32,256]{1,0:T(8,128)S(1)} %bitcast.16, bf16[32,256,128]{2,1,0:T(8,128)(2,1)S(1)} %get-tuple-element.12.grads_ref, bf16[16,128,128]{2,1,0:T(8,128)(2,1)S(1)} %get-tuple-element.13.fold_ref, s32[32,256]{1,0:T(8,128)S(1)} %bitcast.18, ...), custom_call_target="tpu_custom_call" | custom-call | tf_op jit(solution)/shard_map/tail/pallas_call | solution.py:682
  108.2 2.7 %store.1 = (bf16[32,512,128]{2,1,0:T(8,128)(2,1)}, bf16[8192,128]{1,0:T(8,128)(2,1)}) custom-call(bf16[32,512,128]{2,1,0:T(8,128)(2,1)S(1)} %bitcast.14, bf16[8192,128]{1,0:T(8,128)(2,1)S(1)} %get-tuple-element.15.large_ref), custom_call_target="tpu_custom_call" | custom-call | tf_op jit(solution)/shard_map/store/pallas_call | solution.py:720
Async XLA Ops:
  0.6 22.1 %copy-start.2 = (bf16[1304,1024]{1,0:T(8,128)(2,1)S(1)}, bf16[1304,1024]{1,0:T(8,128)(2,1)}, u32[]{:S(2)}) copy-start(bf16[1304,1024]{1,0:T(8,128)(2,1)} %w_ref.1) | copy-start | bytes 8011780
  0.6 22.1 %copy-start.7 = (bf16[256,128]{1,0:T(8,128)(2,1)S(1)}, bf16[256,128]{1,0:T(8,128)(2,1)}, u32[]{:S(2)}) copy-start(bf16[256,128]{1,0:T(8,128)(2,1)} %dense_ref.1) | copy-start | bytes 196612
  0.7 22.1 %copy-start.9 = (s32[16,32]{1,0:T(8,128)S(1)}, s32[16,32]{1,0:T(8,128)}, u32[]{:S(2)}) copy-start(s32[16,32]{1,0:T(8,128)} %sizes_ref.1) | copy-start | bytes 6148
  0.7 22.1 %copy-start.10 = (f32[1024]{0:T(1024)S(1)}, f32[1024]{0:T(1024)}, u32[]{:S(2)}) copy-start(f32[1024]{0:T(1024)} %param.20) | copy-start | bytes 12292
  0.7 22.1 %copy-start.11 = (f32[1024]{0:T(1024)S(1)}, f32[1024]{0:T(1024)}, u32[]{:S(2)}) copy-start(f32[1024]{0:T(1024)} %param.21) | copy-start | bytes 12292
  0.7 22.1 %copy-start.12 = (s32[256]{0:T(256)S(1)}, s32[256]{0:T(256)}, u32[]{:S(2)}) copy-start(s32[256]{0:T(256)} %param.13) | copy-start | bytes 3076
  0.7 42.2 %copy-start.1 = (bf16[1,8192,128]{2,1,0:T(8,128)(2,1)S(1)}, bf16[1,8192,128]{2,1,0:T(8,128)(2,1)}, u32[]{:S(2)}) copy-start(bf16[1,8192,128]{2,1,0:T(8,128)(2,1)} %param.15) | copy-start | bytes 6291460
  22.8 1.6 %copy-start.3 = (bf16[32,256,128]{2,1,0:T(8,128)(2,1)S(1)}, bf16[32,256,128]{2,1,0:T(8,128)(2,1)}, u32[]{:S(2)}) copy-start(bf16[32,256,128]{2,1,0:T(8,128)(2,1)} %get-tuple-element.10.small_ref) | copy-start | bytes 6291460
  24.4 1.0 copy-start.4
  25.4 17.5 %copy-start = (bf16[32,512,128]{2,1,0:T(8,128)(2,1)S(1)}, bf16[32,512,128]{2,1,0:T(8,128)(2,1)}, u32[]{:S(2)}) copy-start(bf16[32,512,128]{2,1,0:T(8,128)(2,1)} %tables_hbm.1) | copy-start | bytes 12582916
  25.4 17.5 %copy-start.5 = (s32[256,32]{0,1:T(8,128)S(1)}, s32[256,32]{0,1:T(8,128)}, u32[]{:S(2)}) copy-start(s32[256,32]{0,1:T(8,128)} %param.12) | copy-start | bytes 98308
  25.4 17.5 %copy-start.6 = (s32[1,32,256]{2,1,0:T(8,128)S(1)}, s32[1,32,256]{2,1,0:T(8,128)}, u32[]{:S(2)}) copy-start(s32[1,32,256]{2,1,0:T(8,128)} %param.18) | copy-start | bytes 98308
  25.4 17.5 %copy-start.8 = (s32[1,32,128]{2,1,0:T(8,128)S(1)}, s32[1,32,128]{2,1,0:T(8,128)}, u32[]{:S(2)}) copy-start(s32[1,32,128]{2,1,0:T(8,128)} %param.17) | copy-start | bytes 49156

commit v5 on v4

--- a/solution.py
+++ b/solution.py
@@ -48,7 +48,7 @@
 
 
 def top_kernel(
-    vec_count, group, pad, index_ref, sizes_ref, dense_ref, labels_ref, small_ref, large_ref,
+    vec_count, group, pad, hook, index_ref, sizes_ref, dense_ref, labels_ref, small_ref, large_ref,
     w_ref, bias_ref, wout_ref, small_out, fold_out, vecs, gram, pairs, spread,
 ):
     batch, width = dense_ref.shape
@@ -57,6 +57,7 @@
     pair_pad = pairs.shape[1]
     pair_count = vec_count * (vec_count - 1) // 2
     scale = width ** (-0.5)
+    index = index_ref[0] if hook is None else position()
     spans = spans_of(vec_count)
 
     def rows_of(i):
@@ -68,7 +69,7 @@
     sample = iota((batch, bag_span), 0)
     bag = iota((batch, bag_span), 1) * batch
     for f in range(feats):
-        reach = sample * sizes_ref[f, index_ref[0]]
+        reach = sample * sizes_ref[f, index]
         hot = ((reach >= bag) & (reach < bag + batch)).astype(f32).astype(bf16)
         vecs[rows_of(1 + small_count + f), :] = jnp.dot(
             hot, large_ref[f], preferred_element_type=f32
@@ -181,14 +182,16 @@
     sample_lane = iota((bag_span, batch), 1)
     bag_row = iota((bag_span, batch), 0) * batch
     for f in range(feats):
-        reach = sample_lane * sizes_ref[f, index_ref[0]]
+        if hook is not None and f == feats // 4:
+            hook()
+        reach = sample_lane * sizes_ref[f, index]
         hot = ((reach >= bag_row) & (reach < bag_row + batch)).astype(f32).astype(bf16)
         fold_out[f] = jnp.dot(
             hot, vecs[rows_of(1 + small_count + f), :].astype(bf16), preferred_element_type=f32
         ).astype(bf16)
 
 
-def top(index, sizes, dense, labels, small, large, w_first, bias, wout):
+def top_plan(dense, small, large):
     batch, width = dense.shape
     small_count, feats, bag_span = small.shape[0], large.shape[0], large.shape[1]
     vec_count = 1 + small_count + feats
@@ -205,8 +208,19 @@
         pltpu.VMEM((batch, pair_pad), bf16),
         pltpu.VMEM((batch, pair_pad), f32),
     ]
+    return vec_count, group, pad, scratch
+
+
+def position():
+    return lax.axis_index("rep") * lax.axis_size("shard") + lax.axis_index("shard")
+
+
+def top(index, sizes, dense, labels, small, large, w_first, bias, wout):
+    batch, width = dense.shape
+    small_count, feats, bag_span = small.shape[0], large.shape[0], large.shape[1]
+    vec_count, group, pad, scratch = top_plan(dense, small, large)
     return pl.pallas_call(
-        functools.partial(top_kernel, vec_count, group, pad),
+        functools.partial(top_kernel, vec_count, group, pad, None),
         out_shape=(
             jax.ShapeDtypeStruct((small_count, batch, width), bf16),
             jax.ShapeDtypeStruct((feats, bag_span, width), bf16),
@@ -338,8 +352,22 @@
     )(rows, ends, ids, table, tables)
 
 
+def swap_copies(ids_ref, grads_ref, peer_ids, peer_grads, sends, recvs):
+    rep, me = lax.axis_index("rep"), lax.axis_index("shard")
+    core = lax.rem(me, 2)
+    peer = me + 1 - 2 * core
+    count = ids_ref.shape[0] // 2
+    away = (1 - core) * count
+    return [
+        remote(
+            ids_ref.at[pl.ds(pl.multiple_of(away, 8), count)], peer_ids, sends.at[0], recvs.at[0], rep, peer
+        ),
+        remote(grads_ref.at[pl.ds(away, count)], peer_grads, sends.at[1], recvs.at[1], rep, peer),
+    ]
+
+
 def tail_kernel(
-    ids_ref, grads_ref, fold_ref, rows_ref, ends_ref, table_ref, tables_ref, small_out, large_out,
+    outs, ids_ref, grads_ref, fold_ref, rows_ref, ends_ref, table_ref, tables_ref, small_out, large_out,
     peer_ids, peer_grads, folds, acc, lhs_0, lhs_1, rhs_0, rhs_1, keep, sent, came, sent_2, came_2, sent_3, came_3,
     prior, local, peer_s, peer_r, fold_s, fold_r, far_s, far_r, rs1_s, rs1_r, rs2_s, rs2_r,
     rs3_s, rs3_r, ag_z, ag_1, ag_2, ag_core, ag_r,
@@ -370,11 +398,7 @@
         lax.fori_loop(low, high, body, 0)
 
     peer = shard_of(z, y, 1 - core)
-    away = (1 - core) * half_count
-    swap = [
-        remote(ids_ref.at[pl.ds(pl.multiple_of(away, 8), half_count)], peer_ids, peer_s.at[0], peer_r.at[0], rep, peer),
-        remote(grads_ref.at[pl.ds(away, half_count)], peer_grads, peer_s.at[1], peer_r.at[1], rep, peer),
-    ]
+    swap = swap_copies(ids_ref, grads_ref, peer_ids, peer_grads, peer_s, peer_r)
 
     def out_block(k):
         to = lax.rem(me + k, groups)
@@ -394,9 +418,10 @@
 
     own_far = remote(fold_ref.at[me], folds.at[rep * groups + me], far_s.at[0], far_r.at[0], other, me)
 
-    greet_all()
-    for copy in swap:
-        copy.start()
+    if outs is None:
+        greet_all()
+        for copy in swap:
+            copy.start()
     loop(1, groups, lambda k: out_block(k).start())
     own_far.start()
     fetch = [
@@ -618,6 +643,17 @@
             second(h, k, rep, z_at, y)
             third(h, k, rep, z_at, y)
             last(h, k, rep, z_at, y)
+    put = []
+
+    def leave(src, dst):
+        if outs is not None:
+            copy = pltpu.make_async_copy(src, dst, outs[2].at[len(put)])
+            copy.start()
+            put.append(copy)
+
+    small_hbm, large_hbm = (None, None) if outs is None else outs[:2]
+    if outs is not None:
+        leave(large_out, large_hbm)
     for k in range(ring):
         z_at = lax.rem(z + ring - k, ring)
         for h in range(2):
@@ -634,14 +670,21 @@
                 where = (rep if k < ring else other, z_at, 1 - y)
             arrived(h, *where, core)
             last(h, 2 * ring + k, *where)
+    if outs is not None:
+        leave(small_out.at[core], small_hbm.at[core])
     for r in range(2):
         for k in range(ring):
             for y_at in range(2):
                 for h in range(2):
                     arrived(h, r, k, y_at, 1 - core)
+        if outs is not None:
+            for h in range(2):
+                leave(small_out.at[1 - core, h, r], small_hbm.at[1 - core, h, r])
 
     for copy in pending + swap:
         copy.wait_send()
+    for copy in put:
+        copy.wait()
     own_far.wait_send()
     loop(1, groups, lambda k: out_block(k).wait_send())
     loop(1, groups, lambda k: far_out(k).wait_send())
@@ -651,7 +694,7 @@
         loop(1, ring, lambda k: third_hop(h, k).wait_send())
 
 
-def tail(ids, grads, fold, rows, ends, table, tables):
+def tail_plan(ids, grads, fold, rows, table, tables):
     groups = fold.shape[0]
     devices, slots = rows.shape
     ring = groups // 4
@@ -679,20 +722,26 @@
         pltpu.VMEM((2, part, width), bf16),
     ]
     dma = pltpu.SemaphoreType.DMA
+    sems = [
+        dma((3,)), dma((2,)), dma((2,)),
+        dma((groups,)), dma((groups,)), dma((groups,)), dma((groups,)),
+        dma((2, 2)), dma((2, 2)), dma((2,)), dma((2,)), dma((2, ring)), dma((2, ring)),
+        dma((2, ring)), dma((2, ring)), dma((2, 2 * ring)), dma((2, 4 * ring)), dma((2, devices)),
+    ]
+    return split, scratch, sems
+
+
+def tail(ids, grads, fold, rows, ends, table, tables):
+    split, scratch, sems = tail_plan(ids, grads, fold, rows, table, tables)
     small, large = pl.pallas_call(
-        tail_kernel,
+        functools.partial(tail_kernel, None),
         out_shape=(
             jax.ShapeDtypeStruct(split, bf16),
             jax.ShapeDtypeStruct(table.shape, bf16),
         ),
         in_specs=[whole(pltpu.VMEM)] * 6 + [whole(pl.ANY)],
         out_specs=(whole(pltpu.VMEM),) * 2,
-        scratch_shapes=scratch + [
-            dma((3,)), dma((2,)), dma((2,)),
-            dma((groups,)), dma((groups,)), dma((groups,)), dma((groups,)),
-            dma((2, 2)), dma((2, 2)), dma((2,)), dma((2,)), dma((2, ring)), dma((2, ring)),
-            dma((2, ring)), dma((2, ring)), dma((2, 2 * ring)), dma((2, 4 * ring)), dma((2, devices)),
-        ],
+        scratch_shapes=scratch + sems,
         compiler_params=pltpu.CompilerParams(
             collective_id=1, has_side_effects=True,
             vmem_limit_bytes=grant(ids, grads, fold, rows, ends, table, table, tables, *scratch),
@@ -702,18 +751,26 @@
     return small.reshape(tables.shape), large
 
 
-def store_kernel(small_ref, large_ref, small_out, large_out, sems):
-    pieces = 4
+def store_kernel(small_ref, large_ref, small_out, large_out, small, large, sems):
+    pieces = sems.shape[2]
     copies = []
-    for n, (src, dst) in enumerate(((small_ref, small_out), (large_ref, large_out))):
+    for n, (src, mid, dst) in enumerate(
+        ((small_ref, small, small_out), (large_ref, large, large_out))
+    ):
         size = src.shape[0] // pieces
         for p in range(pieces):
             at = pl.ds(p * size, size)
-            copies.append(pltpu.make_async_copy(src.at[at], dst.at[at], sems.at[n, p]))
-    for copy in copies:
-        copy.start()
-    for copy in copies:
-        copy.wait()
+            copies.append((
+                pltpu.make_async_copy(src.at[at], mid.at[at], sems.at[0, n, p]),
+                pltpu.make_async_copy(mid.at[at], dst.at[at], sems.at[1, n, p]),
+            ))
+    for come, _ in copies:
+        come.start()
+    for come, go in copies:
+        come.wait()
+        go.start()
+    for _, go in copies:
+        go.wait()
 
 
 def store(small, large):
@@ -723,12 +780,94 @@
             jax.ShapeDtypeStruct(small.shape, small.dtype),
             jax.ShapeDtypeStruct(large.shape, large.dtype),
         ),
-        in_specs=[whole(pltpu.VMEM)] * 2,
-        out_specs=(whole(pl.ANY),) * 2,
-        scratch_shapes=[pltpu.SemaphoreType.DMA((2, 4))],
-        compiler_params=pltpu.CompilerParams(vmem_limit_bytes=16 * 1024 * 1024),
+        in_specs=[whole(pltpu.HBM)] * 2,
+        out_specs=(whole(pltpu.HBM),) * 2,
+        scratch_shapes=[
+            pltpu.VMEM(small.shape, small.dtype), pltpu.VMEM(large.shape, large.dtype),
+            pltpu.SemaphoreType.DMA((2, 2, 8)),
+        ],
+        compiler_params=pltpu.CompilerParams(vmem_limit_bytes=63 * MIB),
         name="store",
     )(small, large)
+
+
+def whole_kernel(plan, counts, *refs):
+    vec_count, group, pad = plan
+    inputs, refs = refs[:12], refs[12:]
+    rows_hbm, ends_hbm, ids_hbm, table_hbm, tables_hbm, split_hbm = inputs[:6]
+    small_hbm, large_hbm, refs = refs[0], refs[1], refs[2:]
+    rows, sizes, refs = refs[0], refs[1], refs[2:]
+    own, refs = refs[: counts[0]], refs[counts[0] :]
+    (rows_v, ends, ids, narrow, tables, by_sample, outbox, large, small, dense, labels, w, bias, wout,
+     grads, fold) = own
+    tops, refs = refs[: counts[1]], refs[counts[1] :]
+    send, recv, local, more, done, small_new, large_new = refs[:7]
+    refs = refs[7:]
+    wide = tops[1].at[pl.ds(0, table_hbm.shape[0])]
+    arrays = tuple(zip(inputs[6:], (sizes, dense, labels, w, bias, wout))) + ((rows_hbm, rows_v),)
+    fetch = [pltpu.make_async_copy(src, dst, more.at[n]) for n, (src, dst) in enumerate(arrays)]
+    for copy in fetch:
+        copy.start()
+    head_kernel(
+        rows_hbm, ends_hbm, ids_hbm, table_hbm, tables_hbm, large, small,
+        rows, ends, ids, narrow, wide, tables, by_sample, outbox, send, recv, local,
+    )
+    for copy in fetch:
+        copy.wait()
+    scratch, sems = refs[: counts[2]], refs[counts[2] :]
+
+    def hook():
+        for copy in swap_copies(ids, grads, scratch[0], scratch[1], sems[1], sems[2]):
+            copy.start()
+
+    top_kernel(
+        vec_count, group, pad, hook, None, sizes, dense, labels, small, large, w, bias, wout,
+        grads, fold, *tops,
+    )
+    tail_kernel(
+        (small_hbm, large_hbm, done), ids, grads, fold, rows_v, ends, narrow, split_hbm,
+        small_new, large_new, *scratch, *sems
+    )
+
+
+def together(rows, ends, ids, table, tables, sizes, dense, labels, w_first, bias, wout, groups):
+    labels, bias, wout = labels[None, :], bias[None, :], wout[None, :]
+    batch, width = dense.shape
+    large = jax.ShapeDtypeStruct((groups, ends.shape[1], width), bf16)
+    small = jax.ShapeDtypeStruct((tables.shape[0], batch, width), bf16)
+    vec_count, group, pad, tops = top_plan(dense, small, large)
+    split, scratch, sems = tail_plan(ids, small, large, rows, table, tables)
+    shaped = (rows, ends, ids, table, tables)
+    own = [pltpu.VMEM(a.shape, a.dtype) for a in shaped]
+    own.append(pltpu.VMEM((batch, tables.shape[0]), ids.dtype))
+    own += [
+        pltpu.VMEM(a.shape, a.dtype)
+        for a in (large, large, small, dense, labels, w_first, bias, wout, small, large)
+    ]
+    need = size_of(*own, *tops, *scratch) + 5 * MIB
+    if need + size_of(table, tables) > 62 * MIB or tops[1].shape[0] < table.shape[0]:
+        return None
+    dma = pltpu.SemaphoreType.DMA
+    small_new, large_new = pl.pallas_call(
+        functools.partial(whole_kernel, (vec_count, group, pad), (len(own), len(tops), len(scratch))),
+        out_shape=(
+            jax.ShapeDtypeStruct(split, bf16),
+            jax.ShapeDtypeStruct(table.shape, bf16),
+        ),
+        in_specs=[whole(pltpu.HBM)] * 12,
+        out_specs=(whole(pltpu.HBM),) * 2,
+        scratch_shapes=[pltpu.SMEM(rows.shape, rows.dtype), pltpu.SMEM(sizes.shape, sizes.dtype)]
+        + own + tops + [dma((groups,)), dma((groups,)), dma((5,)), dma((7,)), dma((6,))]
+        + [pltpu.VMEM(split, bf16), pltpu.VMEM(table.shape, bf16)] + scratch + sems,
+        compiler_params=pltpu.CompilerParams(
+            collective_id=3, has_side_effects=True,
+            vmem_limit_bytes=VMEM_LIMIT,
+        ),
+        name="together",
+    )(
+        rows, ends, ids, table, tables, tables.reshape(split), sizes, dense, labels, w_first, bias, wout
+    )
+    return small_new.reshape(tables.shape), large_new
 
 
 def shards(
@@ -740,6 +879,12 @@
     ends, rows, table = bag_ends[0], owner_row_index[0], large_tables[0]
     ids = jnp.transpose(small_ids)
 
+    both = together(
+        rows, ends, ids, table, small_tables, batch_sizes, dense, labels, w_first, b_first, w_out, groups
+    )
+    if both is not None:
+        small_new, large_new = store(*both)
+        return small_new, large_new[None]
     large, small = head(groups, rows, ends, ids, table, small_tables, w_first)
     small_grads, fold = top(
         index[None], batch_sizes, dense, labels, small, large, w_first, b_first, w_out

time: 113 us -> 110 us (0.973)
  local copies, waits for them, and re-layouts: 2.67 us -> 0 us
    pallas_call x1, Pallas kernels: 2.72 us -> 5.51 us  [store(): pl.pallas_call(store_kernel, out_shape=(jax.ShapeDtypeStruct(small.shape,...]
    unnamed x26 -> x0, local copies, waits for them, and re-layouts: 2.67 us -> none
    pallas_call x3 -> x1, Pallas kernels: 105 us -> 102 us  [together(): pl.pallas_call(functools.partial(whole_kernel, (vec_count, group, pad), (...]
where the time goes in v5:
time: 110 us; the launch traced here: 108 us
  Pallas kernels  108 us (98%)
    pallas_call x1, Pallas kernels, together(): pl.pallas_call(functools.partial(whole_kernel, (vec_count, group, pad), (...  102 us
    pallas_call x1, Pallas kernels, store(): pl.pallas_call(store_kernel, out_shape=(jax.ShapeDtypeStruct(small.shape,...  5.51 us

profile of v5, /device:TPU:1, one launch (start us, length us, event | category | flops | bytes accessed | tf_op | source)
XLA Modules:
  0.0 108.3 jit_solution(3095595345193186082)
XLA Ops:
  0.6 102.0 %together.1 = (bf16[2,2,2,2,4,256,128]{6,5,4,3,2,1,0:T(8,128)(2,1)}, bf16[8192,128]{1,0:T(8,128)(2,1)}) custom-call(s32[32,256]{1,0:T(8,128)} %bitcast.13, s32[32,128]{1,0:T(8,128)} %bitcast.15, s32[32,256]{1,0:T(8,128)} %bitcast.14, bf16[8192,128]{1,0:T(8,128)(2,1)} %bitcast.12, bf16[32,512,128]{2,1,0:T(8,128)(2,1)} %refs_4_.1, ...), custom_call_target="tpu_custom_call" | custom-call | tf_op jit(solution)/shard_map/together/pallas_call | solution.py:851
  102.6 5.5 %store.1 = (bf16[32,512,128]{2,1,0:T(8,128)(2,1)}, bf16[8192,128]{1,0:T(8,128)(2,1)}) custom-call(bf16[32,512,128]{2,1,0:T(8,128)(2,1)} %bitcast.11, bf16[8192,128]{1,0:T(8,128)(2,1)} %get-tuple-element.7.large_ref), custom_call_target="tpu_custom_call" | custom-call | tf_op jit(solution)/shard_map/store/pallas_call | solution.py:777

commit v6 on v5

--- a/solution.py
+++ b/solution.py
@@ -636,8 +636,12 @@
             table_ref[at, :].astype(f32) - step_size * acc[:, q * width : (q + 1) * width]
         ).astype(bf16)
 
+    line = [lax.rem(z + ring - k, ring) for k in range(ring)]
+    if ring == 4:
+        side = z // 2
+        line = [z, z + 1 - 2 * lax.rem(z, 2), 2 - side, 3 * (1 - side)]
     for k in range(1, ring):
-        z_at = lax.rem(z + ring - k, ring)
+        z_at = line[k]
         for h in range(2):
             arrived(h, rep, z_at, y, core)
             second(h, k, rep, z_at, y)
@@ -655,14 +659,14 @@
     if outs is not None:
         leave(large_out, large_hbm)
     for k in range(ring):
-        z_at = lax.rem(z + ring - k, ring)
+        z_at = line[k]
         for h in range(2):
             where = (rep, z_at, 1 - y) if h == 0 else (other, z_at, y)
             arrived(h, *where, core)
             third(h, ring + k, *where)
             last(h, ring + k, *where)
     for k in range(2 * ring):
-        z_at = lax.rem(z + ring - k % ring, ring)
+        z_at = line[k % ring]
         for h in range(2):
             if h == 0:
                 where = (other, z_at, y if k < ring else 1 - y)

time: 110 us -> 110 us (level); the launches traced: 108 us -> 110 us
    pallas_call x1, Pallas kernels: 102 us -> 103 us  [together(): pl.pallas_call(functools.partial(whole_kernel, (vec_count, group, pad), (...]
where the time goes in v6:
time: 110 us
  Pallas kernels  109 us (99%)
    pallas_call x1, Pallas kernels, together(): pl.pallas_call(functools.partial(whole_kernel, (vec_count, group, pad), (...  103 us
    pallas_call x1, Pallas kernels, store(): pl.pallas_call(store_kernel, out_shape=(jax.ShapeDtypeStruct(small.shape,...  5.51 us

profile of v6, /device:TPU:1, one launch (start us, length us, event | category | flops | bytes accessed | tf_op | source)
XLA Modules:
  0.0 109.7 jit_solution(960683423215856097)
XLA Ops:
  0.6 103.4 %together.1 = (bf16[2,2,2,2,4,256,128]{6,5,4,3,2,1,0:T(8,128)(2,1)}, bf16[8192,128]{1,0:T(8,128)(2,1)}) custom-call(s32[32,256]{1,0:T(8,128)} %bitcast.13, s32[32,128]{1,0:T(8,128)} %bitcast.15, s32[32,256]{1,0:T(8,128)} %bitcast.14, bf16[8192,128]{1,0:T(8,128)(2,1)} %bitcast.12, bf16[32,512,128]{2,1,0:T(8,128)(2,1)} %refs_4_.1, ...), custom_call_target="tpu_custom_call" | custom-call | tf_op jit(solution)/shard_map/together/pallas_call | solution.py:855
  104.0 5.5 %store.1 = (bf16[32,512,128]{2,1,0:T(8,128)(2,1)}, bf16[8192,128]{1,0:T(8,128)(2,1)}) custom-call(bf16[32,512,128]{2,1,0:T(8,128)(2,1)} %bitcast.11, bf16[8192,128]{1,0:T(8,128)(2,1)} %get-tuple-element.7.large_ref), custom_call_target="tpu_custom_call" | custom-call | tf_op jit(solution)/shard_map/store/pallas_call | solution.py:781
